TPU v7x, 64 devices: a 2x2x8 block of a 4x4x8 slice. The times are simulated.
64 devices in a mesh: dp: 4 (over x, y), cp: 16 (over z, core).
Axes of the slice: x: 2, y: 2, z: 8, core: 2. Of those that a mesh axis runs over, the one named last changes fastest.
The devices are a block of a 4x4x8 slice.
Arguments:
- x_in: bfloat16 [8192, 1536], P(('dp', 'cp')), parts along dimension 0
- cache_k1: bfloat16 [65536, 2, 128], P(('dp', 'cp')), parts along dimension 0
- cache_v1: bfloat16 [65536, 2, 128], P(('dp', 'cp')), parts along dimension 0
- w_q1: bfloat16 [1536, 1536], replicated
- b_q1: bfloat16 [1536], replicated
- w_k1: bfloat16 [1536, 256], replicated
- b_k1: bfloat16 [256], replicated
- w_v1: bfloat16 [1536, 256], replicated
- w_o1: bfloat16 [1536, 1536], replicated
- w_gate: bfloat16 [1536, 8960], replicated
- w_up: bfloat16 [1536, 8960], replicated
- w_down: bfloat16 [8960, 1536], replicated
- cache_k2: bfloat16 [65536, 2, 128], P(('dp', 'cp')), parts along dimension 0
- cache_v2: bfloat16 [65536, 2, 128], P(('dp', 'cp')), parts along dimension 0
- w_q2: bfloat16 [1536, 1536], replicated
- b_q2: bfloat16 [1536], replicated
- w_k2: bfloat16 [1536, 256], replicated
- b_k2: bfloat16 [256], replicated
- w_v2: bfloat16 [1536, 256], replicated
- w_o2: bfloat16 [1536, 1536], replicated
Outputs:
- output 1: bfloat16 [8192, 1536], P(('dp', 'cp')), parts along dimension 0
- output 2: bfloat16 [8192, 1536], P(('dp', 'cp')), parts along dimension 0
- output 3: bfloat16 [8192, 2, 128], P(('dp', 'cp')), parts along dimension 0
- output 4: bfloat16 [8192, 2, 128], P(('dp', 'cp')), parts along dimension 0
- output 5: bfloat16 [8192, 2, 128], P(('dp', 'cp')), parts along dimension 0
- output 6: bfloat16 [8192, 2, 128], P(('dp', 'cp')), parts along dimension 0
There are 4 independent parts. A program takes and returns all parts, laid end to end along the dimension named above; an argument that names none is the same for every part.
All inputs are finite; a program needn't handle non-finite values.
Results may differ from a plain program's by a relative error of at most 0.0143816.
Values are sent between devices in bfloat16 or wider.
A program may use at most 768 MiB of HBM per device.

v0:
```python
import jax
import jax.numpy as jnp
from jax import lax
from jax.sharding import PartitionSpec as P

ROPE_THETA = 500000.0
NORM_EPS = 1e-5


def rms_norm(vals):
    wide = vals.astype(jnp.float32)
    return (wide * lax.rsqrt(jnp.mean(wide * wide, axis=-1, keepdims=True) + NORM_EPS)).astype(jnp.bfloat16)


def rope_tables(positions, head_dim):
    half_dim = head_dim // 2
    inv_freq = 1.0 / (ROPE_THETA ** (jnp.arange(half_dim, dtype=jnp.float32) * (2.0 / head_dim)))
    angles = positions.astype(jnp.float32)[:, None] * inv_freq[None, :]
    return jnp.cos(angles)[:, None, :], jnp.sin(angles)[:, None, :]


def apply_rope(vals, cos_t, sin_t):
    half_dim = vals.shape[-1] // 2
    first = vals[..., :half_dim]
    second = vals[..., half_dim:]
    return jnp.concatenate([first * cos_t - second * sin_t, second * cos_t + first * sin_t], axis=-1)


def project_rows(layer_in, w_q, b_q, w_k, b_k, w_v, positions, head_dim):
    rows = layer_in.shape[0]
    cos_t, sin_t = rope_tables(positions, head_dim)
    q_pre = (jnp.dot(layer_in, w_q, preferred_element_type=jnp.float32) + b_q.astype(jnp.float32)).astype(jnp.bfloat16)
    k_pre = (jnp.dot(layer_in, w_k, preferred_element_type=jnp.float32) + b_k.astype(jnp.float32)).astype(jnp.bfloat16)
    v_new = jnp.dot(layer_in, w_v, preferred_element_type=jnp.float32).astype(jnp.bfloat16).reshape(rows, -1, head_dim)
    q_rot = apply_rope(q_pre.reshape(rows, -1, head_dim).astype(jnp.float32), cos_t, sin_t).astype(jnp.bfloat16)
    k_new = apply_rope(k_pre.reshape(rows, -1, head_dim).astype(jnp.float32), cos_t, sin_t).astype(jnp.bfloat16)
    return q_rot, k_new, v_new


def mlp_block(resid_h, w_gate, w_up, w_down):
    normed = rms_norm(resid_h)
    gate_act = jnp.dot(normed, w_gate, preferred_element_type=jnp.float32).astype(jnp.bfloat16)
    up_proj = jnp.dot(normed, w_up, preferred_element_type=jnp.float32).astype(jnp.bfloat16)
    mixed = (jax.nn.silu(gate_act.astype(jnp.float32)) * up_proj.astype(jnp.float32)).astype(jnp.bfloat16)
    return (resid_h.astype(jnp.float32) + jnp.dot(mixed, w_down, preferred_element_type=jnp.float32)).astype(jnp.bfloat16)


def partial_attend(q_grp, keys, values, scale, visible):
    scores = jnp.einsum('tkgd,skd->tkgs', q_grp, keys, preferred_element_type=jnp.float32) * scale
    if visible is not None:
        scores = jnp.where(visible, scores, -jnp.inf)
    peak = jnp.max(scores, axis=-1)
    prob_w = jnp.exp(scores - peak[..., None])
    total = jnp.sum(prob_w, axis=-1)
    summed = jnp.einsum('tkgs,skd->tkgd', prob_w.astype(jnp.bfloat16), values, preferred_element_type=jnp.float32)
    return summed / total[..., None], peak + jnp.log(total)


def merge_parts(out_a, lse_a, out_b, lse_b):
    lse_new = jnp.logaddexp(lse_a, lse_b)
    merged = out_a * jnp.exp(lse_a - lse_new)[..., None] + out_b * jnp.exp(lse_b - lse_new)[..., None]
    return merged, lse_new


def attention_layer(layer_in, cache_k, cache_v, w_q, b_q, w_k, b_k, w_v, w_o, axis_size):
    tok_dev = layer_in.shape[0]
    cache_dev, kv_heads, head_dim = cache_k.shape
    heads = w_q.shape[1] // head_dim
    my_idx = lax.axis_index('cp')
    positions = axis_size * cache_dev + my_idx * tok_dev + jnp.arange(tok_dev)
    q_rot, k_new, v_new = project_rows(layer_in, w_q, b_q, w_k, b_k, w_v, positions, head_dim)
    q_grp = q_rot.reshape(tok_dev, kv_heads, heads // kv_heads, head_dim)
    scale = head_dim ** -0.5
    all_k = lax.all_gather(k_new, 'cp', axis=0, tiled=True)
    all_v = lax.all_gather(v_new, 'cp', axis=0, tiled=True)
    q_pos = my_idx * tok_dev + jnp.arange(tok_dev)
    visible = (jnp.arange(axis_size * tok_dev)[None, :] <= q_pos[:, None])[:, None, None, :]
    out_acc, lse_acc = partial_attend(q_grp, all_k, all_v, scale, visible)
    out_loc, lse_loc = partial_attend(q_grp, cache_k, cache_v, scale, None)
    out_acc, lse_acc = merge_parts(out_acc, lse_acc, out_loc, lse_loc)
    shift = [(src_idx, (src_idx + 1) % axis_size) for src_idx in range(axis_size)]

    def cache_step(step, carry):
        blk_k, blk_v, out_run, lse_run = carry
        blk_k = lax.ppermute(blk_k, 'cp', shift)
        blk_v = lax.ppermute(blk_v, 'cp', shift)
        out_blk, lse_blk = partial_attend(q_grp, blk_k, blk_v, scale, None)
        out_run, lse_run = merge_parts(out_run, lse_run, out_blk, lse_blk)
        return blk_k, blk_v, out_run, lse_run

    carry_end = lax.fori_loop(0, axis_size - 1, cache_step, (cache_k, cache_v, out_acc, lse_acc))
    o_half = carry_end[2].astype(jnp.bfloat16).reshape(tok_dev, heads * head_dim)
    y_out = jnp.dot(o_half, w_o, preferred_element_type=jnp.float32).astype(jnp.bfloat16)
    return y_out, k_new, v_new


def solution(mesh):
    axis_size = mesh.shape['cp']
    rows_spec = P(('dp', 'cp'), None)
    cache_spec = P(('dp', 'cp'), None, None)
    mat_spec = P(None, None)
    vec_spec = P(None)
    layer_specs = (cache_spec, cache_spec, mat_spec, vec_spec, mat_spec, vec_spec, mat_spec, mat_spec)
    in_specs = (rows_spec,) + layer_specs + (mat_spec, mat_spec, mat_spec) + layer_specs
    out_specs = (rows_spec, rows_spec, cache_spec, cache_spec, cache_spec, cache_spec)

    def forward(x_in, cache_k1, cache_v1, w_q1, b_q1, w_k1, b_k1, w_v1, w_o1, w_gate, w_up, w_down, cache_k2, cache_v2, w_q2, b_q2, w_k2, b_k2, w_v2, w_o2):
        y_one, k_one, v_one = attention_layer(x_in, cache_k1, cache_v1, w_q1, b_q1, w_k1, b_k1, w_v1, w_o1, axis_size)
        resid_h = (x_in.astype(jnp.float32) + y_one.astype(jnp.float32)).astype(jnp.bfloat16)
        hidden = mlp_block(resid_h, w_gate, w_up, w_down)
        y_two, k_two, v_two = attention_layer(rms_norm(hidden), cache_k2, cache_v2, w_q2, b_q2, w_k2, b_k2, w_v2, w_o2, axis_size)
        return hidden, y_two, k_one, v_one, k_two, v_two

    return jax.shard_map(forward, mesh=mesh, in_specs=in_specs, out_specs=out_specs, check_vma=False)
```

profile of v0, /device:TPU:22, one launch (start us, length us, event | category | flops | bytes accessed | tf_op | source)
XLA Modules:
  0.0 779.2 jit_solution(18262621654098603286)
XLA Ops:
  24.6 25.4 %all-gather.7.cloned.1.call-done = bf16[2048,2,128]{2,0,1:T(8,128)(2,1)} async-done(((bf16[128,2,128]{2,0,1:T(8,128)(2,1)}), bf16[2048,2,128]{2,0,1:T(8,128)(2,1)}) %all-gather.7.cloned.1.call-update) | async-done | bytes 1048592 | tf_op jit(solution)/shard_map/all_gather | solution.py:74
  57.6 27.0 %all-gather.5.cloned.1.call-done = bf16[2048,2,128]{0,2,1:T(8,128)(2,1)} async-done(((bf16[128,2,128]{0,2,1:T(8,128)(2,1)}), bf16[2048,2,128]{0,2,1:T(8,128)(2,1)}) %all-gather.5.cloned.1.call-update) | async-done | bytes 1048592 | tf_op jit(solution)/shard_map/all_gather | solution.py:75
  95.9 275.4 %while.32 = (s32[]{:T(128)}, bf16[1024,2,128]{2,0,1:T(8,128)(2,1)S(1)}, bf16[1024,2,128]{2,0,1:T(8,128)(2,1)}, f32[128,2,6,128]{3,0,2,1:T(8,128)S(1)}, f32[128,2...) while((s32[]{:T(128)}, bf16[1024,2,128]{2,0,1:T(8,128)(2,1)S(1)}, ...), condition=%wide.region_7.8_spmd, body=%wide.region_4.7_spmd.sunk | while | flops 818691072 | bytes 28278940 | solution.py:91
  132.8 9.7 %collective-permute-done = bf16[1024,2,128]{2,0,1:T(8,128)(2,1)S(1)} collective-permute-done((bf16[1024,2,128]{2,0,1:T(8,128)(2,1)S(1)}, bf16[1024,2,128]{2,0,1:T(8,128)(2,1)S(1)}, u32[]{:S(2)}, u32[]{:S(2)}) %collective-permute-start) | collective-permute-done | bytes 524320 | tf_op jit(solution)/shard_map/while/body/eval_jaxpr/ppermute | solution.py:85
  151.1 9.7 %collective-permute-done = bf16[1024,2,128]{2,0,1:T(8,128)(2,1)S(1)} collective-permute-done((bf16[1024,2,128]{2,0,1:T(8,128)(2,1)S(1)}, bf16[1024,2,128]{2,0,1:T(8,128)(2,1)S(1)}, u32[]{:S(2)}, u32[]{:S(2)}) %collective-permute-start) | collective-permute-done | bytes 524320 | tf_op jit(solution)/shard_map/while/body/eval_jaxpr/ppermute | solution.py:85
  169.5 9.7 %collective-permute-done = bf16[1024,2,128]{2,0,1:T(8,128)(2,1)S(1)} collective-permute-done((bf16[1024,2,128]{2,0,1:T(8,128)(2,1)S(1)}, bf16[1024,2,128]{2,0,1:T(8,128)(2,1)S(1)}, u32[]{:S(2)}, u32[]{:S(2)}) %collective-permute-start) | collective-permute-done | bytes 524320 | tf_op jit(solution)/shard_map/while/body/eval_jaxpr/ppermute | solution.py:85
  187.9 9.7 %collective-permute-done = bf16[1024,2,128]{2,0,1:T(8,128)(2,1)S(1)} collective-permute-done((bf16[1024,2,128]{2,0,1:T(8,128)(2,1)S(1)}, bf16[1024,2,128]{2,0,1:T(8,128)(2,1)S(1)}, u32[]{:S(2)}, u32[]{:S(2)}) %collective-permute-start) | collective-permute-done | bytes 524320 | tf_op jit(solution)/shard_map/while/body/eval_jaxpr/ppermute | solution.py:85
  206.2 9.7 %collective-permute-done = bf16[1024,2,128]{2,0,1:T(8,128)(2,1)S(1)} collective-permute-done((bf16[1024,2,128]{2,0,1:T(8,128)(2,1)S(1)}, bf16[1024,2,128]{2,0,1:T(8,128)(2,1)S(1)}, u32[]{:S(2)}, u32[]{:S(2)}) %collective-permute-start) | collective-permute-done | bytes 524320 | tf_op jit(solution)/shard_map/while/body/eval_jaxpr/ppermute | solution.py:85
  224.6 9.7 %collective-permute-done = bf16[1024,2,128]{2,0,1:T(8,128)(2,1)S(1)} collective-permute-done((bf16[1024,2,128]{2,0,1:T(8,128)(2,1)S(1)}, bf16[1024,2,128]{2,0,1:T(8,128)(2,1)S(1)}, u32[]{:S(2)}, u32[]{:S(2)}) %collective-permute-start) | collective-permute-done | bytes 524320 | tf_op jit(solution)/shard_map/while/body/eval_jaxpr/ppermute | solution.py:85
  242.9 9.7 %collective-permute-done = bf16[1024,2,128]{2,0,1:T(8,128)(2,1)S(1)} collective-permute-done((bf16[1024,2,128]{2,0,1:T(8,128)(2,1)S(1)}, bf16[1024,2,128]{2,0,1:T(8,128)(2,1)S(1)}, u32[]{:S(2)}, u32[]{:S(2)}) %collective-permute-start) | collective-permute-done | bytes 524320 | tf_op jit(solution)/shard_map/while/body/eval_jaxpr/ppermute | solution.py:85
  261.3 9.7 %collective-permute-done = bf16[1024,2,128]{2,0,1:T(8,128)(2,1)S(1)} collective-permute-done((bf16[1024,2,128]{2,0,1:T(8,128)(2,1)S(1)}, bf16[1024,2,128]{2,0,1:T(8,128)(2,1)S(1)}, u32[]{:S(2)}, u32[]{:S(2)}) %collective-permute-start) | collective-permute-done | bytes 524320 | tf_op jit(solution)/shard_map/while/body/eval_jaxpr/ppermute | solution.py:85
  279.7 9.7 %collective-permute-done = bf16[1024,2,128]{2,0,1:T(8,128)(2,1)S(1)} collective-permute-done((bf16[1024,2,128]{2,0,1:T(8,128)(2,1)S(1)}, bf16[1024,2,128]{2,0,1:T(8,128)(2,1)S(1)}, u32[]{:S(2)}, u32[]{:S(2)}) %collective-permute-start) | collective-permute-done | bytes 524320 | tf_op jit(solution)/shard_map/while/body/eval_jaxpr/ppermute | solution.py:85
  298.0 9.7 %collective-permute-done = bf16[1024,2,128]{2,0,1:T(8,128)(2,1)S(1)} collective-permute-done((bf16[1024,2,128]{2,0,1:T(8,128)(2,1)S(1)}, bf16[1024,2,128]{2,0,1:T(8,128)(2,1)S(1)}, u32[]{:S(2)}, u32[]{:S(2)}) %collective-permute-start) | collective-permute-done | bytes 524320 | tf_op jit(solution)/shard_map/while/body/eval_jaxpr/ppermute | solution.py:85
  316.4 9.7 %collective-permute-done = bf16[1024,2,128]{2,0,1:T(8,128)(2,1)S(1)} collective-permute-done((bf16[1024,2,128]{2,0,1:T(8,128)(2,1)S(1)}, bf16[1024,2,128]{2,0,1:T(8,128)(2,1)S(1)}, u32[]{:S(2)}, u32[]{:S(2)}) %collective-permute-start) | collective-permute-done | bytes 524320 | tf_op jit(solution)/shard_map/while/body/eval_jaxpr/ppermute | solution.py:85
  334.7 9.7 %collective-permute-done = bf16[1024,2,128]{2,0,1:T(8,128)(2,1)S(1)} collective-permute-done((bf16[1024,2,128]{2,0,1:T(8,128)(2,1)S(1)}, bf16[1024,2,128]{2,0,1:T(8,128)(2,1)S(1)}, u32[]{:S(2)}, u32[]{:S(2)}) %collective-permute-start) | collective-permute-done | bytes 524320 | tf_op jit(solution)/shard_map/while/body/eval_jaxpr/ppermute | solution.py:85
  353.1 9.7 %collective-permute-done = bf16[1024,2,128]{2,0,1:T(8,128)(2,1)S(1)} collective-permute-done((bf16[1024,2,128]{2,0,1:T(8,128)(2,1)S(1)}, bf16[1024,2,128]{2,0,1:T(8,128)(2,1)S(1)}, u32[]{:S(2)}, u32[]{:S(2)}) %collective-permute-start) | collective-permute-done | bytes 524320 | tf_op jit(solution)/shard_map/while/body/eval_jaxpr/ppermute | solution.py:85
  374.8 14.7 %fusion.50 = f32[128,8960]{1,0:T(8,128)} fusion(bf16[1536,8960]{1,0:T(8,128)(2,1)} %param.33, f32[128,1536]{1,0:T(8,128)S(1)} %get-tuple-element.181, f32[128]{0:T(128)S(1)} %add_rsqrt_fusion.1), kind=kOutput, calls=%fused_computation.50 | convolution fusion | flops 3525902336 | bytes 32899584 | tf_op jit(solution)/shard_map/dot_general | solution.py:42
  389.6 21.7 %fusion.145 = (f32[128]{0:T(128)S(1)}, bf16[128,1536]{1,0:T(8,128)(2,1)S(1)}) fusion(f32[128,1536]{1,0:T(8,128)S(1)} %get-tuple-element.181, bf16[8960,1536]{1,0:T(8,128)(2,1)} %param.35, bf16[1536,8960]{1,0:T(8,128)(2,1)} %param.34, f32[128,8960]{1,0:T(8,128)} %fusion.50, f32[128]{0:T(128)S(1)} %add_rsqrt_fusion.1), kind=kOutput, calls=%fused_computation.121 | convolution fusion | flops 7056982016 | bytes 60818432 | tf_op jit(solution)/shard_map/dot_general | solution.py:45
  430.2 17.1 %all-gather.11.cloned.1.call-done = bf16[2048,2,128]{2,0,1:T(8,128)(2,1)} async-done(((bf16[128,2,128]{2,0,1:T(8,128)(2,1)}), bf16[2048,2,128]{2,0,1:T(8,128)(2,1)}) %all-gather.11.cloned.1.call-update) | async-done | bytes 1048592 | tf_op jit(solution)/shard_map/all_gather | solution.py:74
  455.0 26.2 %all-gather.9.cloned.1.call-done = bf16[2048,2,128]{0,2,1:T(8,128)(2,1)} async-done(((bf16[128,2,128]{0,2,1:T(8,128)(2,1)}), bf16[2048,2,128]{0,2,1:T(8,128)(2,1)}) %all-gather.9.cloned.1.call-update) | async-done | bytes 1048592 | tf_op jit(solution)/shard_map/all_gather | solution.py:75
  492.6 275.4 %while.33 = (s32[]{:T(128)}, bf16[1024,2,128]{2,0,1:T(8,128)(2,1)S(1)}, bf16[1024,2,128]{2,0,1:T(8,128)(2,1)}, f32[128,2,6,128]{3,0,2,1:T(8,128)S(1)}, f32[128,2...) while((s32[]{:T(128)}, bf16[1024,2,128]{2,0,1:T(8,128)(2,1)S(1)}, ...), condition=%wide.region_17.18_spmd, body=%wide.region_14.17_spmd.sunk | while | flops 818691072 | bytes 28278940 | solution.py:91
  529.5 9.7 %collective-permute-done.2 = bf16[1024,2,128]{2,0,1:T(8,128)(2,1)S(1)} collective-permute-done((bf16[1024,2,128]{2,0,1:T(8,128)(2,1)S(1)}, bf16[1024,2,128]{2,0,1:T(8,128)(2,1)S(1)}, u32[]{:S(2)}, u32[]{:S(2)}) %collective-permute-start.2) | collective-permute-done | bytes 524320 | tf_op jit(solution)/shard_map/while/body/eval_jaxpr/ppermute | solution.py:85
  584.6 9.7 %collective-permute-done.2 = bf16[1024,2,128]{2,0,1:T(8,128)(2,1)S(1)} collective-permute-done((bf16[1024,2,128]{2,0,1:T(8,128)(2,1)S(1)}, bf16[1024,2,128]{2,0,1:T(8,128)(2,1)S(1)}, u32[]{:S(2)}, u32[]{:S(2)}) %collective-permute-start.2) | collective-permute-done | bytes 524320 | tf_op jit(solution)/shard_map/while/body/eval_jaxpr/ppermute | solution.py:85
  639.7 9.7 %collective-permute-done.2 = bf16[1024,2,128]{2,0,1:T(8,128)(2,1)S(1)} collective-permute-done((bf16[1024,2,128]{2,0,1:T(8,128)(2,1)S(1)}, bf16[1024,2,128]{2,0,1:T(8,128)(2,1)S(1)}, u32[]{:S(2)}, u32[]{:S(2)}) %collective-permute-start.2) | collective-permute-done | bytes 524320 | tf_op jit(solution)/shard_map/while/body/eval_jaxpr/ppermute | solution.py:85
  (449 shorter events, 474.6 us)
Async XLA Ops:
  7.2 42.8 %all-gather.7.cloned.1.call-start = ((), (), s32[]{:S(2)}) async-start(), calls=%async_computation.1 | async-start | bytes 1114112 | tf_op jit(solution)/shard_map/all_gather | solution.py:74
  10.8 73.8 %all-gather.5.cloned.1.call-start = ((), (), s32[]{:S(2)}) async-start(), calls=%async_computation | async-start | bytes 1114112 | tf_op jit(solution)/shard_map/all_gather | solution.py:75
  13.3 434.0 %all-gather.11.cloned.1.call-start = ((), (), s32[]{:S(2)}) async-start(), calls=%async_computation.3 | async-start | bytes 1114112 | tf_op jit(solution)/shard_map/all_gather | solution.py:74
  114.4 15.4 %collective-permute-start.1 = (bf16[1024,2,128]{2,0,1:T(8,128)(2,1)}, bf16[1024,2,128]{2,0,1:T(8,128)(2,1)S(1)}, u32[]{:S(2)}, u32[]{:S(2)}) collective-permute-start(bf16[1024,2,128]{2,0,1:T(8,128)(2,1)} %get-tuple-element.287), channel_id=1, source_target_pairs={{0,1},{1,2},{2,3},{3,4},{4,5},{5,6},{6,7},{7,8},{8,9},{9,10},{10,1... | collective-permute-start | bytes 1572872 | tf_op jit(solution)/shard_map/while/body/eval_jaxpr/ppermute | solution.py:86
  132.7 15.4 %collective-permute-start.1 = (bf16[1024,2,128]{2,0,1:T(8,128)(2,1)}, bf16[1024,2,128]{2,0,1:T(8,128)(2,1)S(1)}, u32[]{:S(2)}, u32[]{:S(2)}) collective-permute-start(bf16[1024,2,128]{2,0,1:T(8,128)(2,1)} %get-tuple-element.287), channel_id=1, source_target_pairs={{0,1},{1,2},{2,3},{3,4},{4,5},{5,6},{6,7},{7,8},{8,9},{9,10},{10,1... | collective-permute-start | bytes 1572872 | tf_op jit(solution)/shard_map/while/body/eval_jaxpr/ppermute | solution.py:86
  151.1 15.4 %collective-permute-start.1 = (bf16[1024,2,128]{2,0,1:T(8,128)(2,1)}, bf16[1024,2,128]{2,0,1:T(8,128)(2,1)S(1)}, u32[]{:S(2)}, u32[]{:S(2)}) collective-permute-start(bf16[1024,2,128]{2,0,1:T(8,128)(2,1)} %get-tuple-element.287), channel_id=1, source_target_pairs={{0,1},{1,2},{2,3},{3,4},{4,5},{5,6},{6,7},{7,8},{8,9},{9,10},{10,1... | collective-permute-start | bytes 1572872 | tf_op jit(solution)/shard_map/while/body/eval_jaxpr/ppermute | solution.py:86
  169.4 15.4 %collective-permute-start.1 = (bf16[1024,2,128]{2,0,1:T(8,128)(2,1)}, bf16[1024,2,128]{2,0,1:T(8,128)(2,1)S(1)}, u32[]{:S(2)}, u32[]{:S(2)}) collective-permute-start(bf16[1024,2,128]{2,0,1:T(8,128)(2,1)} %get-tuple-element.287), channel_id=1, source_target_pairs={{0,1},{1,2},{2,3},{3,4},{4,5},{5,6},{6,7},{7,8},{8,9},{9,10},{10,1... | collective-permute-start | bytes 1572872 | tf_op jit(solution)/shard_map/while/body/eval_jaxpr/ppermute | solution.py:86
  187.8 15.4 %collective-permute-start.1 = (bf16[1024,2,128]{2,0,1:T(8,128)(2,1)}, bf16[1024,2,128]{2,0,1:T(8,128)(2,1)S(1)}, u32[]{:S(2)}, u32[]{:S(2)}) collective-permute-start(bf16[1024,2,128]{2,0,1:T(8,128)(2,1)} %get-tuple-element.287), channel_id=1, source_target_pairs={{0,1},{1,2},{2,3},{3,4},{4,5},{5,6},{6,7},{7,8},{8,9},{9,10},{10,1... | collective-permute-start | bytes 1572872 | tf_op jit(solution)/shard_map/while/body/eval_jaxpr/ppermute | solution.py:86
  206.2 15.4 %collective-permute-start.1 = (bf16[1024,2,128]{2,0,1:T(8,128)(2,1)}, bf16[1024,2,128]{2,0,1:T(8,128)(2,1)S(1)}, u32[]{:S(2)}, u32[]{:S(2)}) collective-permute-start(bf16[1024,2,128]{2,0,1:T(8,128)(2,1)} %get-tuple-element.287), channel_id=1, source_target_pairs={{0,1},{1,2},{2,3},{3,4},{4,5},{5,6},{6,7},{7,8},{8,9},{9,10},{10,1... | collective-permute-start | bytes 1572872 | tf_op jit(solution)/shard_map/while/body/eval_jaxpr/ppermute | solution.py:86
  242.9 15.4 %collective-permute-start.1 = (bf16[1024,2,128]{2,0,1:T(8,128)(2,1)}, bf16[1024,2,128]{2,0,1:T(8,128)(2,1)S(1)}, u32[]{:S(2)}, u32[]{:S(2)}) collective-permute-start(bf16[1024,2,128]{2,0,1:T(8,128)(2,1)} %get-tuple-element.287), channel_id=1, source_target_pairs={{0,1},{1,2},{2,3},{3,4},{4,5},{5,6},{6,7},{7,8},{8,9},{9,10},{10,1... | collective-permute-start | bytes 1572872 | tf_op jit(solution)/shard_map/while/body/eval_jaxpr/ppermute | solution.py:86
  261.2 15.4 %collective-permute-start.1 = (bf16[1024,2,128]{2,0,1:T(8,128)(2,1)}, bf16[1024,2,128]{2,0,1:T(8,128)(2,1)S(1)}, u32[]{:S(2)}, u32[]{:S(2)}) collective-permute-start(bf16[1024,2,128]{2,0,1:T(8,128)(2,1)} %get-tuple-element.287), channel_id=1, source_target_pairs={{0,1},{1,2},{2,3},{3,4},{4,5},{5,6},{6,7},{7,8},{8,9},{9,10},{10,1... | collective-permute-start | bytes 1572872 | tf_op jit(solution)/shard_map/while/body/eval_jaxpr/ppermute | solution.py:86
  298.0 15.4 %collective-permute-start.1 = (bf16[1024,2,128]{2,0,1:T(8,128)(2,1)}, bf16[1024,2,128]{2,0,1:T(8,128)(2,1)S(1)}, u32[]{:S(2)}, u32[]{:S(2)}) collective-permute-start(bf16[1024,2,128]{2,0,1:T(8,128)(2,1)} %get-tuple-element.287), channel_id=1, source_target_pairs={{0,1},{1,2},{2,3},{3,4},{4,5},{5,6},{6,7},{7,8},{8,9},{9,10},{10,1... | collective-permute-start | bytes 1572872 | tf_op jit(solution)/shard_map/while/body/eval_jaxpr/ppermute | solution.py:86
  316.3 15.4 %collective-permute-start.1 = (bf16[1024,2,128]{2,0,1:T(8,128)(2,1)}, bf16[1024,2,128]{2,0,1:T(8,128)(2,1)S(1)}, u32[]{:S(2)}, u32[]{:S(2)}) collective-permute-start(bf16[1024,2,128]{2,0,1:T(8,128)(2,1)} %get-tuple-element.287), channel_id=1, source_target_pairs={{0,1},{1,2},{2,3},{3,4},{4,5},{5,6},{6,7},{7,8},{8,9},{9,10},{10,1... | collective-permute-start | bytes 1572872 | tf_op jit(solution)/shard_map/while/body/eval_jaxpr/ppermute | solution.py:86
  353.0 15.4 %collective-permute-start.1 = (bf16[1024,2,128]{2,0,1:T(8,128)(2,1)}, bf16[1024,2,128]{2,0,1:T(8,128)(2,1)S(1)}, u32[]{:S(2)}, u32[]{:S(2)}) collective-permute-start(bf16[1024,2,128]{2,0,1:T(8,128)(2,1)} %get-tuple-element.287), channel_id=1, source_target_pairs={{0,1},{1,2},{2,3},{3,4},{4,5},{5,6},{6,7},{7,8},{8,9},{9,10},{10,1... | collective-permute-start | bytes 1572872 | tf_op jit(solution)/shard_map/while/body/eval_jaxpr/ppermute | solution.py:86
  412.8 68.4 %all-gather.9.cloned.1.call-start = ((), (), s32[]{:S(2)}) async-start(), calls=%async_computation.2 | async-start | bytes 1114112 | tf_op jit(solution)/shard_map/all_gather | solution.py:75
  511.1 15.4 %collective-permute-start.3 = (bf16[1024,2,128]{2,0,1:T(8,128)(2,1)}, bf16[1024,2,128]{2,0,1:T(8,128)(2,1)S(1)}, u32[]{:S(2)}, u32[]{:S(2)}) collective-permute-start(bf16[1024,2,128]{2,0,1:T(8,128)(2,1)} %get-tuple-element.308), channel_id=1, source_target_pairs={{0,1},{1,2},{2,3},{3,4},{4,5},{5,6},{6,7},{7,8},{8,9},{9,10},{10,1... | collective-permute-start | bytes 1572872 | tf_op jit(solution)/shard_map/while/body/eval_jaxpr/ppermute | solution.py:86
  529.5 15.4 %collective-permute-start.3 = (bf16[1024,2,128]{2,0,1:T(8,128)(2,1)}, bf16[1024,2,128]{2,0,1:T(8,128)(2,1)S(1)}, u32[]{:S(2)}, u32[]{:S(2)}) collective-permute-start(bf16[1024,2,128]{2,0,1:T(8,128)(2,1)} %get-tuple-element.308), channel_id=1, source_target_pairs={{0,1},{1,2},{2,3},{3,4},{4,5},{5,6},{6,7},{7,8},{8,9},{9,10},{10,1... | collective-permute-start | bytes 1572872 | tf_op jit(solution)/shard_map/while/body/eval_jaxpr/ppermute | solution.py:86
  547.8 15.4 %collective-permute-start.3 = (bf16[1024,2,128]{2,0,1:T(8,128)(2,1)}, bf16[1024,2,128]{2,0,1:T(8,128)(2,1)S(1)}, u32[]{:S(2)}, u32[]{:S(2)}) collective-permute-start(bf16[1024,2,128]{2,0,1:T(8,128)(2,1)} %get-tuple-element.308), channel_id=1, source_target_pairs={{0,1},{1,2},{2,3},{3,4},{4,5},{5,6},{6,7},{7,8},{8,9},{9,10},{10,1... | collective-permute-start | bytes 1572872 | tf_op jit(solution)/shard_map/while/body/eval_jaxpr/ppermute | solution.py:86
  566.2 15.4 %collective-permute-start.3 = (bf16[1024,2,128]{2,0,1:T(8,128)(2,1)}, bf16[1024,2,128]{2,0,1:T(8,128)(2,1)S(1)}, u32[]{:S(2)}, u32[]{:S(2)}) collective-permute-start(bf16[1024,2,128]{2,0,1:T(8,128)(2,1)} %get-tuple-element.308), channel_id=1, source_target_pairs={{0,1},{1,2},{2,3},{3,4},{4,5},{5,6},{6,7},{7,8},{8,9},{9,10},{10,1... | collective-permute-start | bytes 1572872 | tf_op jit(solution)/shard_map/while/body/eval_jaxpr/ppermute | solution.py:86
  602.9 15.4 %collective-permute-start.3 = (bf16[1024,2,128]{2,0,1:T(8,128)(2,1)}, bf16[1024,2,128]{2,0,1:T(8,128)(2,1)S(1)}, u32[]{:S(2)}, u32[]{:S(2)}) collective-permute-start(bf16[1024,2,128]{2,0,1:T(8,128)(2,1)} %get-tuple-element.308), channel_id=1, source_target_pairs={{0,1},{1,2},{2,3},{3,4},{4,5},{5,6},{6,7},{7,8},{8,9},{9,10},{10,1... | collective-permute-start | bytes 1572872 | tf_op jit(solution)/shard_map/while/body/eval_jaxpr/ppermute | solution.py:86
  621.3 15.4 %collective-permute-start.3 = (bf16[1024,2,128]{2,0,1:T(8,128)(2,1)}, bf16[1024,2,128]{2,0,1:T(8,128)(2,1)S(1)}, u32[]{:S(2)}, u32[]{:S(2)}) collective-permute-start(bf16[1024,2,128]{2,0,1:T(8,128)(2,1)} %get-tuple-element.308), channel_id=1, source_target_pairs={{0,1},{1,2},{2,3},{3,4},{4,5},{5,6},{6,7},{7,8},{8,9},{9,10},{10,1... | collective-permute-start | bytes 1572872 | tf_op jit(solution)/shard_map/while/body/eval_jaxpr/ppermute | solution.py:86
  658.0 15.4 %collective-permute-start.3 = (bf16[1024,2,128]{2,0,1:T(8,128)(2,1)}, bf16[1024,2,128]{2,0,1:T(8,128)(2,1)S(1)}, u32[]{:S(2)}, u32[]{:S(2)}) collective-permute-start(bf16[1024,2,128]{2,0,1:T(8,128)(2,1)} %get-tuple-element.308), channel_id=1, source_target_pairs={{0,1},{1,2},{2,3},{3,4},{4,5},{5,6},{6,7},{7,8},{8,9},{9,10},{10,1... | collective-permute-start | bytes 1572872 | tf_op jit(solution)/shard_map/while/body/eval_jaxpr/ppermute | solution.py:86
  676.3 15.4 %collective-permute-start.3 = (bf16[1024,2,128]{2,0,1:T(8,128)(2,1)}, bf16[1024,2,128]{2,0,1:T(8,128)(2,1)S(1)}, u32[]{:S(2)}, u32[]{:S(2)}) collective-permute-start(bf16[1024,2,128]{2,0,1:T(8,128)(2,1)} %get-tuple-element.308), channel_id=1, source_target_pairs={{0,1},{1,2},{2,3},{3,4},{4,5},{5,6},{6,7},{7,8},{8,9},{9,10},{10,1... | collective-permute-start | bytes 1572872 | tf_op jit(solution)/shard_map/while/body/eval_jaxpr/ppermute | solution.py:86
  713.0 15.4 %collective-permute-start.3 = (bf16[1024,2,128]{2,0,1:T(8,128)(2,1)}, bf16[1024,2,128]{2,0,1:T(8,128)(2,1)S(1)}, u32[]{:S(2)}, u32[]{:S(2)}) collective-permute-start(bf16[1024,2,128]{2,0,1:T(8,128)(2,1)} %get-tuple-element.308), channel_id=1, source_target_pairs={{0,1},{1,2},{2,3},{3,4},{4,5},{5,6},{6,7},{7,8},{8,9},{9,10},{10,1... | collective-permute-start | bytes 1572872 | tf_op jit(solution)/shard_map/while/body/eval_jaxpr/ppermute | solution.py:86
  (68 other events, 1030.5 us)
Sparse Core Ops, SparseCore 0:
  10.9 39.0 all-gather.6
  52.1 32.4 all-gather.4
  412.9 34.3 all-gather.10
  448.7 32.4 all-gather.8
where the time goes:
time: 787 us; the launch traced here: 779 us
  waiting for transfers between devices  487 us (62%)
  matrix products  179 us (23%)
  other arithmetic  46.9 us (6%)
  local copies, waits for them, and re-layouts  40 us (5%)
  between operations  15 us (2%)
  starting transfers between devices  8.8 us (1%)
    ppermute x30, waiting for transfers between devices, cache_step(): blk_k = lax.ppermute(blk_k, 'cp', shift)  287 us
    ppermute x30, waiting for transfers between devices, cache_step(): blk_v = lax.ppermute(blk_v, 'cp', shift)  105 us
    dot_general x34, matrix products, partial_attend(): jnp.einsum('tkgs,skd->tkgd', prob_w.astype(jnp.bfloat16), values, preferr...  84.2 us
    all_gather x2, waiting for transfers between devices, attention_layer(): all_v = lax.all_gather(v_new, 'cp', axis=0, tiled=True)  53.2 us
    all_gather x2, waiting for transfers between devices, attention_layer(): all_k = lax.all_gather(k_new, 'cp', axis=0, tiled=True)  42.5 us
    reduce_sum x34, other arithmetic, partial_attend(): total = jnp.sum(prob_w, axis=-1)  41.7 us
    dot_general x34, matrix products, partial_attend(): jnp.einsum('tkgd,skd->tkgs', q_grp, keys, preferred_element_type=jnp.floa...  40.3 us
    while x60, local copies, waits for them, and re-layouts  24.6 us
  transfers between devices with their start and end apart: 64, of which 64 were waited for; matrix products, arithmetic and copies ran while one was open for 13% of the time, Pallas kernels for 0%

commit v1 on v0

v1 whole, which is shorter than its diff:
```python
import functools

import jax
import jax.numpy as jnp
import numpy as np
from jax import lax
from jax.experimental import pallas as pl
from jax.experimental.pallas import tpu as pltpu
from jax.sharding import PartitionSpec as P

ROPE_THETA = 500000.0
NORM_EPS = 1e-5
LOG2E = 1.4426950408889634
BF16 = jnp.bfloat16
F32 = jnp.float32
FF_TILE = 640
W_SLOTS = 3


def rms_norm(wide):
    return (wide * lax.rsqrt(jnp.mean(wide * wide, axis=-1, keepdims=True) + NORM_EPS)).astype(BF16)


def block_kernel(n, x_ref, kc1, vc1, kc2, vc2, wq1, wk1, wv1, wo1, wg, wu, wd, wq2, wk2, wv2, wo2, bias_ref, local_rot, base_rot,
                 g_out, y_out, app_out,
                 kv, nkv, raw, snd, wide, sbuf, cos_ref, sin_ref, knew, vnew, app_in, app_buf,
                 xb, hb, qb, acc, m_s, l_s, ob, gacc, grecv, ybuf, wqkv, wob, w13, w2b,
                 ring_s, ring_r, new_s, new_r, d2d_s, d2d_r, loc, wsem):
    nz = n // 2
    far = nz // 2
    n_arr = 4 * (far - 1) + 2
    n_new = 2 * (far - 1) + 1
    cp = lax.axis_index("cp")
    c = lax.rem(cp, 2)
    z = lax.div(cp, 2)
    partner = cp + 1 - 2 * c
    tok = x_ref.shape[0]
    heads_dev = qb.shape[0]
    hd = qb.shape[1]
    pair = 2 * tok
    cache_dev = kv.shape[4]
    n_steps = n_arr + 2
    half = heads_dev * hd
    ff_half = wg.shape[1] // 2
    tiles = ff_half // FF_TILE
    cache = (kc1, vc1), (kc2, vc2)
    wqkv_src = (wq1, wk1, wv1), (wq2, wk2, wv2)
    wo_src = (wo1, wo2)
    score_mul = hd ** -0.5 * LOG2E

    def toward(direction):
        return {"cp": lax.rem(cp + n + 2 - 4 * direction, n)}

    barrier = pltpu.get_barrier_semaphore()
    for other in (partner, lax.rem(cp + 2, n), lax.rem(cp + n - 2, n)):
        pl.semaphore_signal(barrier, inc=1, device_id={"cp": other})
    pl.semaphore_wait(barrier, 3)

    def load_cache(layer, j):
        return pltpu.make_async_copy(cache[layer][j], raw.at[layer, j], loc.at[1 + 2 * layer + j])

    def swap_cache(layer):
        return pltpu.make_async_remote_copy(snd.at[layer], kv.at[layer, z, c], d2d_s.at[1 + layer], d2d_r.at[1 + layer],
                                            device_id={"cp": partner})

    def split_cache(layer):
        for j in range(2):
            def one_block(b, carry):
                wide[...] = raw[layer, j, pl.ds(pl.multiple_of(b * 2 * hd, 2 * hd), 2 * hd)].astype(F32)
                first = wide[pl.ds(0, hd, stride=2)]
                second = wide[pl.ds(1, hd, stride=2)]
                mine = jnp.where(c == 0, first, second)
                theirs = jnp.where(c == 0, second, first)
                if j == 1:
                    mine, theirs = mine.T, theirs.T
                rows = pl.ds(pl.multiple_of(b * hd, hd), hd)
                kv[layer, z, c, j, rows] = mine.astype(BF16)
                snd[layer, j, rows] = theirs.astype(BF16)
                return carry
            lax.fori_loop(0, cache_dev // hd, one_block, 0)

    own_rows = pl.ds(pl.multiple_of(c * tok, tok), tok)
    other_rows = pl.ds(pl.multiple_of((1 - c) * tok, tok), tok)
    load_x = pltpu.make_async_copy(x_ref, xb.at[own_rows], loc.at[0])
    swap_x = pltpu.make_async_remote_copy(x_ref, xb.at[own_rows], d2d_s.at[0], d2d_r.at[0], device_id={"cp": partner})

    def load_wqkv(layer):
        w_q, w_k, w_v = wqkv_src[layer]
        return (pltpu.make_async_copy(w_q.at[:, pl.ds(pl.multiple_of(c * half, hd), half)], wqkv.at[:, pl.ds(0, half)], loc.at[5]),
                pltpu.make_async_copy(w_k.at[:, pl.ds(pl.multiple_of(c * hd, hd), hd)], wqkv.at[:, pl.ds(half, hd)], loc.at[6]),
                pltpu.make_async_copy(w_v.at[:, pl.ds(pl.multiple_of(c * hd, hd), hd)], wqkv.at[:, pl.ds(half + hd, hd)], loc.at[7]))

    def load_wo(layer):
        return pltpu.make_async_copy(wo_src[layer], wob, loc.at[8])

    def load_ff(tile, slot):
        cols = pl.ds(pl.multiple_of(c * ff_half + tile * FF_TILE, 128), FF_TILE)
        return (pltpu.make_async_copy(wg.at[:, cols], w13.at[slot, :, pl.ds(0, FF_TILE)], wsem.at[slot, 0]),
                pltpu.make_async_copy(wu.at[:, cols], w13.at[slot, :, pl.ds(FF_TILE, FF_TILE)], wsem.at[slot, 1]),
                pltpu.make_async_copy(wd.at[cols], w2b.at[slot], wsem.at[slot, 2]))

    for j in range(2):
        load_cache(0, j).start()
    load_x.start()
    swap_x.start()
    for cpy in load_wqkv(0):
        cpy.start()

    def piece_of(t):
        dist = lax.div(t, 4) + 1
        r = lax.rem(t, 4)
        direction = lax.rem(t, 2)
        order = lax.div(r, 2) + lax.rem(r, 2) * lax.div(dist, far)
        src = lax.rem(z + nz + dist * (2 * direction - 1), nz)
        return src, lax.rem(c + order, 2), direction

    def ring_copy(layer, src, piece, t, direction):
        return pltpu.make_async_remote_copy(kv.at[layer, src, piece], kv.at[layer, src, piece],
                                            ring_s.at[layer, t], ring_r.at[layer, t], device_id=toward(direction))

    def send_own(layer, order):
        for direction in range(2):
            ring_copy(layer, z, lax.rem(c + order, 2), 2 * order + direction, direction).start()

    def arrive(layer, t):
        src, piece, direction = piece_of(t)
        ring_copy(layer, src, piece, t, direction).wait_recv()
        last = 4 * (far - 1)

        @pl.when((t < last - 4) | (t == last - 4) | (t == last - 1))
        def _():
            ring_copy(layer, src, piece, t + 4 - 2 * lax.div(t, last - 1), direction).start()

    def new_piece(u):
        dist = lax.div(u, 2) + 1
        direction = lax.rem(u, 2)
        src_raw = z + dist * (2 * direction - 1)
        return lax.rem(src_raw + nz, nz), direction

    def new_copy(layer, src, u, direction):
        return pltpu.make_async_remote_copy(nkv.at[layer, src], nkv.at[layer, src],
                                            new_s.at[layer, u], new_r.at[layer, u], device_id=toward(direction))

    def attend(k_view, v_view, causal):
        keys = k_view.shape[0]
        kb = min(256, keys)
        blocks = keys // kb

        def scores(h):
            top = None
            for b in range(blocks):
                s = jnp.dot(k_view[b * kb:(b + 1) * kb], qb[h], preferred_element_type=F32)
                if causal:
                    key = lax.broadcasted_iota(jnp.int32, s.shape, 0) + b * kb
                    query = lax.broadcasted_iota(jnp.int32, s.shape, 1)
                    s = jnp.where(key <= query, s, -jnp.inf)
                sbuf[h % 2, b * kb:(b + 1) * kb] = s
                part = jnp.max(s.reshape(kb // 8, 8, pair), axis=0)
                top = part if top is None else jnp.maximum(top, part)
            return top

        top = scores(0)
        for h in range(heads_dev):
            top_next = scores(h + 1) if h + 1 < heads_dev else None
            m_old = m_s[h]
            m_new = jnp.maximum(m_old, jnp.max(top, axis=0, keepdims=True))
            alpha = jnp.exp2((m_old - m_new) * score_mul)
            total = l_s[h] * alpha
            added = None
            for b in range(blocks):
                s = sbuf[h % 2, b * kb:(b + 1) * kb].reshape(kb // 8, 8, pair)
                p = jnp.exp2((s - m_new[None]) * score_mul)
                total = total + jnp.sum(p, axis=0)
                v_t = jnp.concatenate([v_view[b * kb + i * hd:b * kb + (i + 1) * hd] for i in range(kb // hd)], axis=1)
                part = jnp.dot(v_t, p.reshape(kb, pair).astype(BF16), preferred_element_type=F32)
                added = part if added is None else added + part
            acc[h] = (acc[h].reshape(hd // 8, 8, pair) * alpha[None]).reshape(hd, pair) + added
            l_s[h] = total
            m_s[h] = m_new
            top = top_next

    def new_arrive(layer, u):
        src, direction = new_piece(u)
        new_copy(layer, src, u, direction).wait_recv()

        @pl.when((u < n_new - 3) | (u == n_new - 3))
        def _():
            new_copy(layer, src, u + 2, direction).start()

        @pl.when(src < z)
        def _():
            attend(nkv.at[layer, src, 0], nkv.at[layer, src, 1], False)

    def clear():
        def one_head(h, carry):
            m_s[h] = jnp.full(m_s.shape[1:], -jnp.inf, F32)
            l_s[h] = jnp.zeros(l_s.shape[1:], F32)
            acc[h] = jnp.zeros(acc.shape[1:], F32)
            return carry
        lax.fori_loop(0, heads_dev, one_head, 0)

    def rope(vals):
        rounded = vals.astype(BF16).astype(F32)
        return rounded * cos_ref[...] + pltpu.roll(rounded, hd // 2, 1) * sin_ref[...]

    def rotation():
        base = base_rot[z]
        cos_ref[...] = base[0:1] * local_rot[0] - base[1:2] * local_rot[1]
        sin_ref[...] = base[3:4] * local_rot[0] + base[2:3] * local_rot[1]

    def project(layer):
        proj = jnp.dot(xb[...], wqkv[...], preferred_element_type=F32)
        start = layer * (bias_ref.shape[0] // 2)
        for h in range(heads_dev):
            cols = slice(h * hd, (h + 1) * hd)
            qb[h] = rope(proj[:, cols] + bias_ref[pl.ds(start + c * heads_dev + h, 1)]).T.astype(BF16)
        k_rot = rope(proj[:, half:half + hd] + bias_ref[pl.ds(start + 2 * heads_dev + c, 1)]).astype(BF16)
        nkv[layer, z, 0] = k_rot
        knew[layer] = k_rot
        v_val = proj[:, half + hd:]
        vnew[layer] = v_val.astype(BF16)
        for i in range(pair // hd):
            nkv[layer, z, 1, i * hd:(i + 1) * hd] = v_val[i * hd:(i + 1) * hd].T.astype(BF16)

    def append_swap(layer, j):
        return pltpu.make_async_remote_copy((knew, vnew)[j].at[layer, other_rows], app_in.at[layer, j],
                                            d2d_s.at[8 + 2 * layer + j], d2d_r.at[8 + 2 * layer + j], device_id={"cp": partner})

    def send_new(layer):
        for direction in range(2):
            new_copy(layer, z, direction, direction).start()
        for j in range(2):
            append_swap(layer, j).start()

    def put_append(layer):
        return pltpu.make_async_copy(app_buf.at[layer], app_out.at[layer], loc.at[9 + layer])

    def append(layer):
        for j in range(2):
            append_swap(layer, j).wait_recv()
            mine = (knew, vnew)[j][layer, own_rows].astype(F32)
            theirs = app_in[layer, j].astype(F32)
            wide[pl.ds(0, tok, stride=2)] = jnp.where(c == 0, mine, theirs)
            wide[pl.ds(1, tok, stride=2)] = jnp.where(c == 0, theirs, mine)
            app_buf[layer, j] = wide[pl.ds(0, 2 * tok)].astype(BF16)
        put_append(layer).start()

    def finish_heads(layer):
        for h in range(heads_dev):
            total = jnp.sum(l_s[h], axis=0, keepdims=True)
            ob[layer, c, :, h * hd:(h + 1) * hd] = (acc[h] / total).T.astype(BF16)

    def attend_layer(layer):
        def step(s, carry):
            if layer == 0:
                @pl.when(s == n_steps - 2)
                def _():
                    send_own(1, 0)
                    send_own(1, 1)

                @pl.when(s >= 2)
                def _():
                    arrive(0, s - 2)
            else:
                @pl.when((s >= 2) & (s < 6))
                def _():
                    arrive(1, s + 2)

                @pl.when(s >= 10)
                def _():
                    arrive(1, s - 2)
            own = 1 - lax.div(s + n_steps - 2, n_steps)
            src, piece, _ = piece_of(lax.rem(s + n_steps - 2, n_steps))
            src = own * z + (1 - own) * src
            piece = own * lax.rem(c + s, 2) + (1 - own) * piece
            attend(kv.at[layer, src, piece, 0], kv.at[layer, src, piece, 1], False)

            @pl.when((s == 5) | (s == 9) | (s == 13) | (s == n_steps - 1))
            def _():
                last = lax.div(s, n_steps - 1)
                lo = lax.div(s - 5, 2) + last

                def new_step(u, carry):
                    new_arrive(layer, u)
                    return carry
                lax.fori_loop(lo, lo + 2 - last, new_step, 0)
            return carry

        lax.fori_loop(0, n_steps, step, 0)

    def span(body, lo, hi):
        def step(i, carry):
            body(i)
            return carry
        lax.fori_loop(lo, hi, step, 0)

    for j in range(2):
        load_cache(0, j).wait()
    split_cache(0)
    swap_cache(0).start()
    send_own(0, 0)
    for j in range(2):
        load_cache(1, j).start()
    rotation()
    swap_cache(0).wait_recv()
    send_own(0, 1)
    load_x.wait()
    swap_x.wait_recv()
    for cpy in load_wqkv(0):
        cpy.wait()
    project(0)
    send_new(0)
    load_wo(0).start()
    for cpy in load_wqkv(1):
        cpy.start()
    for slot in range(W_SLOTS):
        for cpy in load_ff(slot, slot):
            cpy.start()
    clear()
    attend(nkv.at[0, z, 0], nkv.at[0, z, 1], True)
    for j in range(2):
        load_cache(1, j).wait()
    split_cache(1)
    swap_cache(1).start()
    append(0)
    swap_cache(1).wait_recv()
    attend_layer(0)
    finish_heads(0)

    swap_o = pltpu.make_async_remote_copy(ob.at[0, c], ob.at[0, c], d2d_s.at[5], d2d_r.at[5], device_id={"cp": partner})
    swap_o.start()
    load_wo(0).wait()
    swap_o.wait_recv()
    y_one = (jnp.dot(ob[0, 0], wob[:half], preferred_element_type=F32)
             + jnp.dot(ob[0, 1], wob[half:], preferred_element_type=F32)).astype(BF16)
    h_val = (xb[...].astype(F32) + y_one.astype(F32)).astype(BF16)
    hb[...] = h_val
    xb[...] = rms_norm(h_val.astype(F32))
    load_wo(1).start()
    gacc[...] = jnp.zeros(gacc.shape, F32)

    def ff_step(i, carry):
        slot = lax.rem(i, W_SLOTS)
        for cpy in load_ff(i, slot):
            cpy.wait()
        both = jnp.dot(xb[...], w13[slot], preferred_element_type=F32).astype(BF16).astype(F32)
        gate = both[:, :FF_TILE]
        mixed = (gate * jax.nn.sigmoid(gate) * both[:, FF_TILE:]).astype(BF16)
        gacc[...] += jnp.dot(mixed, w2b[slot], preferred_element_type=F32)

        @pl.when(i + W_SLOTS < tiles)
        def _():
            for cpy in load_ff(i + W_SLOTS, slot):
                cpy.start()

        @pl.when(i == tiles // 2)
        def _():
            arrive(1, 0)
            arrive(1, 1)
        return carry

    lax.fori_loop(0, tiles, ff_step, 0)
    swap_g = pltpu.make_async_remote_copy(gacc, grecv, d2d_s.at[7], d2d_r.at[7], device_id={"cp": partner})
    swap_g.start()
    swap_g.wait_recv()
    g_val = (hb[...].astype(F32) + (gacc[...] + grecv[...])).astype(BF16)
    hb[...] = g_val
    put_g = pltpu.make_async_copy(hb.at[own_rows], g_out, loc.at[11])
    put_g.start()
    xb[...] = rms_norm(g_val.astype(F32))
    for cpy in load_wqkv(1):
        cpy.wait()
    project(1)
    span(lambda t: arrive(1, t), 2, 4)
    send_new(1)

    clear()
    attend(nkv.at[1, z, 0], nkv.at[1, z, 1], True)
    append(1)
    attend_layer(1)
    finish_heads(1)
    swap_y = pltpu.make_async_remote_copy(ob.at[1, c, other_rows], ob.at[1, c, other_rows], d2d_s.at[6], d2d_r.at[6],
                                          device_id={"cp": partner})
    swap_y.start()
    load_wo(1).wait()
    swap_y.wait_recv()
    ybuf[...] = (jnp.dot(ob[1, 0, own_rows], wob[:half], preferred_element_type=F32)
                 + jnp.dot(ob[1, 1, own_rows], wob[half:], preferred_element_type=F32)).astype(BF16)
    put_y = pltpu.make_async_copy(ybuf, y_out, loc.at[12])
    put_y.start()

    for layer in range(2):
        put_append(layer).wait()
        swap_cache(layer).wait_send()
        for j in range(2):
            append_swap(layer, j).wait_send()
        span(lambda t: ring_copy(layer, 0, 0, t, 0).wait_send(), 0, n_arr)
        span(lambda u: new_copy(layer, 0, u, 0).wait_send(), 0, n_new)
    swap_x.wait_send()
    swap_o.wait_send()
    swap_g.wait_send()
    swap_y.wait_send()
    put_g.wait()
    put_y.wait()


def rotation_tables(n, tok, cache_dev, hd):
    half_dim = hd // 2
    inv_freq = np.tile(ROPE_THETA ** (-np.arange(half_dim) * (2.0 / hd)), 2)
    pair = 2 * tok
    offset = np.arange(pair)[:, None] * inv_freq[None, :]
    base = (n * cache_dev + np.arange(n // 2) * pair)[:, None] * inv_freq[None, :]
    sign = np.where(np.arange(hd) < half_dim, -1.0, 1.0)[None, :]
    local_rot = np.stack([np.cos(offset), np.sin(offset)])
    base_rot = np.stack([np.cos(base), np.sin(base), sign * np.cos(base), sign * np.sin(base)], axis=1)
    return jnp.asarray(local_rot, F32), jnp.asarray(base_rot, F32)


def copy_kernel(g_in, y_in, app_in, g_out, y_out, *rest):
    app_outs, (g_buf, y_buf, app_buf, sems) = rest[:4], rest[4:]
    ins = [pltpu.make_async_copy(src, buf, sems.at[0, i]) for i, (src, buf) in enumerate(((y_in, y_buf), (g_in, g_buf), (app_in, app_buf)))]
    outs = [[pltpu.make_async_copy(y_buf, y_out, sems.at[1, 0])], [pltpu.make_async_copy(g_buf, g_out, sems.at[1, 1])],
            [pltpu.make_async_copy(app_buf.at[i // 2, i % 2], app_outs[i], sems.at[1, 2 + i]) for i in range(4)]]
    for cpy in ins:
        cpy.start()
    for cpy, group in zip(ins, outs):
        cpy.wait()
        for out in group:
            out.start()
    for group in outs:
        for out in group:
            out.wait()


def hand_over(hidden, y_two, app):
    any_spec = pl.BlockSpec(memory_space=pl.ANY)
    row_shape = jax.ShapeDtypeStruct(hidden.shape, hidden.dtype)
    app_shape = jax.ShapeDtypeStruct(app.shape[2:], app.dtype)
    return pl.pallas_call(
        copy_kernel,
        out_shape=[row_shape, row_shape] + [app_shape] * 4,
        in_specs=[any_spec] * 3,
        out_specs=[any_spec] * 6,
        scratch_shapes=[pltpu.VMEM(hidden.shape, BF16), pltpu.VMEM(hidden.shape, BF16), pltpu.VMEM(app.shape, BF16),
                        pltpu.SemaphoreType.DMA((2, 6))],
        name="hand_over",
    )(hidden, y_two, app)


def fused_blocks(n, x_in, cache, weights, biases, tables):
    tok, d_model = x_in.shape
    cache_dev, kv_heads, hd = cache[0].shape
    w_q1, w_gate = weights[0], weights[4]
    heads_dev = w_q1.shape[1] // hd // kv_heads
    half = heads_dev * hd
    nz = n // 2
    far = nz // 2
    n_arr = 4 * (far - 1) + 2
    n_new = 2 * (far - 1) + 1
    pair = 2 * tok
    rows = [arr.reshape(cache_dev * kv_heads, hd) for arr in cache]
    any_spec = pl.BlockSpec(memory_space=pl.ANY)
    vmem_spec = pl.BlockSpec(memory_space=pltpu.VMEM)
    dma = pltpu.SemaphoreType.DMA
    ff_half = w_gate.shape[1] // 2
    flops = 2 * pair * (d_model * (half + 2 * hd) * 2 + 3 * d_model * ff_half + 2 * half * d_model * 2) + 8 * pair * half * n * cache_dev
    return pl.pallas_call(
        functools.partial(block_kernel, n),
        out_shape=(jax.ShapeDtypeStruct((tok, d_model), BF16), jax.ShapeDtypeStruct((tok, d_model), BF16),
                   jax.ShapeDtypeStruct((2, 2, kv_heads * tok, hd), BF16)),
        in_specs=[any_spec] * 16 + [vmem_spec] * 3,
        out_specs=(any_spec, any_spec, any_spec),
        scratch_shapes=[
            pltpu.VMEM((2, nz, 2, 2, cache_dev, hd), BF16),
            pltpu.VMEM((2, nz, 2, pair, hd), BF16),
            pltpu.VMEM((2, 2, 2 * cache_dev, hd), BF16),
            pltpu.VMEM((2, 2, cache_dev, hd), BF16),
            pltpu.VMEM((2 * hd, hd), F32),
            pltpu.VMEM((2, cache_dev, pair), F32),
            pltpu.VMEM((pair, hd), F32),
            pltpu.VMEM((pair, hd), F32),
            pltpu.VMEM((2, pair, hd), BF16),
            pltpu.VMEM((2, pair, hd), BF16),
            pltpu.VMEM((2, 2, tok, hd), BF16),
            pltpu.VMEM((2, 2, pair, hd), BF16),
            pltpu.VMEM((pair, d_model), BF16),
            pltpu.VMEM((pair, d_model), BF16),
            pltpu.VMEM((heads_dev, hd, pair), BF16),
            pltpu.VMEM((heads_dev, hd, pair), F32),
            pltpu.VMEM((heads_dev, 8, pair), F32),
            pltpu.VMEM((heads_dev, 8, pair), F32),
            pltpu.VMEM((2, 2, pair, half), BF16),
            pltpu.VMEM((pair, d_model), F32),
            pltpu.VMEM((pair, d_model), F32),
            pltpu.VMEM((tok, d_model), BF16),
            pltpu.VMEM((d_model, half + 2 * hd), BF16),
            pltpu.VMEM((2 * half, d_model), BF16),
            pltpu.VMEM((W_SLOTS, d_model, 2 * FF_TILE), BF16),
            pltpu.VMEM((W_SLOTS, FF_TILE, d_model), BF16),
            dma((2, n_arr)), dma((2, n_arr)), dma((2, n_new)), dma((2, n_new)),
            dma((12,)), dma((12,)), dma((13,)), dma((W_SLOTS, 3)),
        ],
        compiler_params=pltpu.CompilerParams(collective_id=0, has_side_effects=True, vmem_limit_bytes=67043328),
        cost_estimate=pl.CostEstimate(flops=flops, bytes_accessed=6 * d_model * ff_half, transcendentals=0),
        name="fused_blocks",
    )(x_in, *rows, *weights, biases, *tables)


def solution(mesh):
    axis_size = mesh.shape['cp']
    rows_spec = P(('dp', 'cp'), None)
    cache_spec = P(('dp', 'cp'), None, None)
    mat_spec = P(None, None)
    vec_spec = P(None)
    layer_specs = (cache_spec, cache_spec, mat_spec, vec_spec, mat_spec, vec_spec, mat_spec, mat_spec)
    in_specs = (rows_spec,) + layer_specs + (mat_spec, mat_spec, mat_spec) + layer_specs
    out_specs = (rows_spec, rows_spec, cache_spec, cache_spec, cache_spec, cache_spec)

    def forward(x_in, cache_k1, cache_v1, w_q1, b_q1, w_k1, b_k1, w_v1, w_o1, w_gate, w_up, w_down, cache_k2, cache_v2, w_q2, b_q2, w_k2, b_k2, w_v2, w_o2):
        tok = x_in.shape[0]
        cache_dev, kv_heads, hd = cache_k1.shape
        tables = rotation_tables(axis_size, tok, cache_dev, hd)
        parts = (b_q1, b_k1, b_q2, b_k2)
        width = sum(part.shape[0] for part in parts)
        biases, start = 0.0, 0
        for part in parts:
            biases = biases + jnp.pad(part.astype(F32), (start, width - start - part.shape[0]))
            start += part.shape[0]
        biases = lax.optimization_barrier(biases).reshape(-1, hd)
        weights = (w_q1, w_k1, w_v1, w_o1, w_gate, w_up, w_down, w_q2, w_k2, w_v2, w_o2)
        hidden, y_two, app = fused_blocks(axis_size, x_in, (cache_k1, cache_v1, cache_k2, cache_v2), weights, biases, tables)
        outs = hand_over(hidden, y_two, app)
        return (outs[0], outs[1], *(arr.reshape(tok, kv_heads, hd) for arr in outs[2:]))

    return jax.shard_map(forward, mesh=mesh, in_specs=in_specs, out_specs=out_specs, check_vma=False)
```

time: 787 us -> 204 us (0.26)
  the two profiles are of different devices: /device:TPU:22 before, /device:TPU:21 now
where the time goes in v1:
time: 204 us
  Pallas kernels  202 us (99%)
    pallas_call x1, Pallas kernels, fused_blocks(): pl.pallas_call(functools.partial(block_kernel, n), out_shape=(jax.ShapeDt...  200 us

profile of v1, /device:TPU:21, one launch (start us, length us, event | category | flops | bytes accessed | tf_op | source)
XLA Modules:
  0.0 204.0 jit_solution(13145315877212394619)
XLA Ops:
  0.6 1.3 convert_add_fusion
  2.0 199.7 %fused_blocks.1 = (bf16[128,1536]{1,0:T(8,128)(2,1)}, bf16[128,1536]{1,0:T(8,128)(2,1)}, bf16[2,2,256,128]{3,2,1,0:T(8,128)(2,1)}) custom-call(bf16[128,1536]{1,0:T(8,128)(2,1)} %x_ref.1, bf16[2048,128]{1,0:T(8,128)(2,1)} %bitcast.10, bf16[2048,128]{1,0:T(8,128)(2,1)} %bitcast.11, bf16[2048,128]{1,0:T(8,128)(2,1)} %bitcast.12, bf16[2048,128]{1,0:T(8,128)(2,1)} %bitcast.13, ...), custom_call_target="tpu_custom_call" | custom-call | flops 40365981696 | bytes 41287680 | tf_op jit(solution)/shard_map/fused_blocks/pallas_call | solution.py:467
  201.7 2.1 %hand_over.1 = (bf16[128,1536]{1,0:T(8,128)(2,1)}, bf16[128,1536]{1,0:T(8,128)(2,1)}, bf16[256,128]{1,0:T(8,128)(2,1)}, bf16[256,128]{1,0:T(8,128)(2,1)}, bf16[2...) custom-call(bf16[128,1536]{1,0:T(8,128)(2,1)} %get-tuple-element.15.g_in, bf16[128,1536]{1,0:T(8,128)(2,1)} %get-tuple-element.16.y_in, ...), custom_call_target="tpu_custom_call" | custom-call | tf_op jit(solution)/shard_map/hand_over/pallas_call | solution.py:439

commit v2 on v1

v2 whole, which is shorter than its diff:
```python
import functools

import jax
import jax.numpy as jnp
import numpy as np
from jax import lax
from jax.experimental import pallas as pl
from jax.experimental.pallas import tpu as pltpu
from jax.sharding import PartitionSpec as P

ROPE_THETA = 500000.0
NORM_EPS = 1e-5
LOG2E = 1.4426950408889634
BF16 = jnp.bfloat16
F32 = jnp.float32
FF_TILE = 640
W_SLOTS = 3
CORES = 2


def parity(i):
    return lax.rem(i, CORES)


def halve(i):
    return lax.div(i, CORES)


def repeat(count, body):
    lax.fori_loop(0, count, body, 0)


def product(left, right):
    return jnp.dot(left, right, preferred_element_type=F32)


def rms_norm(wide):
    return (wide * lax.rsqrt(jnp.mean(wide * wide, axis=-1, keepdims=True) + NORM_EPS)).astype(BF16)


def block_kernel(n, x_ref, kc1, vc1, kc2, vc2, wq1, wk1, wv1, wo1, wg, wu, wd, wq2, wk2, wv2, wo2, bias_ref, local_rot, base_rot,
                 g_out, y_out, app_out,
                 kv1, kv2, nk1, nk2, part_ml, far_acc, far_ml, raw, snd, wide, sbuf, cos_ref, sin_ref, knew, vnew, app_in, app_buf,
                 xb, hb, qb, acc, m_s, l_s, ob, gacc, grecv, ybuf, wqkv, wob, w13, w2b,
                 pair_s, pair_r, ring_s, ring_r, new_s, new_r, d2d_s, d2d_r, loc, wsem):
    nz = n // CORES
    far = nz // CORES
    n_arr = 4 * (far - 1) + 2
    n_new = 2 * (far - 1) + 1
    cp = lax.axis_index("cp")
    c = parity(cp)
    z = halve(cp)
    partner = cp + 1 - 2 * c
    odd = parity(z)
    mate = z + 1 - 2 * odd
    near = lax.rem(z + nz - 1 + 2 * odd, nz)
    tok = x_ref.shape[0]
    heads_dev = qb.shape[1]
    hd = qb.shape[2]
    pair = CORES * tok
    cache_dev = kv1.shape[3]
    n_steps = n_arr + 2
    half = heads_dev * hd
    ff_half = wg.shape[1] // 2
    tiles = ff_half // FF_TILE
    cache = (kc1, vc1), (kc2, vc2)
    wqkv_src = (wq1, wk1, wv1), (wq2, wk2, wv2)
    wo_src = (wo1, wo2)
    score_mul = hd ** -0.5 * LOG2E

    def toward(direction):
        return {"cp": lax.rem(cp + n + 2 - 4 * direction, n)}

    def chip(index):
        return {"cp": 2 * index + c}

    def own_slot(layer):
        return kv1.at[0] if layer == 0 else kv2.at[z]

    def own_new(layer):
        return nk1.at[0] if layer == 0 else nk2.at[z]

    def load_cache(layer, j):
        return pltpu.make_async_copy(cache[layer][j], raw.at[layer, j], loc.at[1 + 2 * layer + j])

    def swap_cache(layer):
        return pltpu.make_async_remote_copy(snd.at[layer], own_slot(layer).at[c], d2d_s.at[1 + layer], d2d_r.at[1 + layer],
                                            device_id={"cp": partner})

    def split_cache(layer):
        for j in range(CORES):
            def one_block(b, carry):
                wide[...] = raw[layer, j, pl.ds(pl.multiple_of(b * 2 * hd, 2 * hd), 2 * hd)].astype(F32)
                first = wide[pl.ds(0, hd, stride=2)]
                second = wide[pl.ds(1, hd, stride=2)]
                mine = jnp.where(c == 0, first, second)
                theirs = jnp.where(c == 0, second, first)
                if j == 1:
                    mine, theirs = mine.T, theirs.T
                rows = pl.ds(pl.multiple_of(b * hd, hd), hd)
                own_slot(layer)[c, j, rows] = mine.astype(BF16)
                snd[layer, j, rows] = theirs.astype(BF16)
                return carry
            repeat(cache_dev // hd, one_block)

    own_rows = pl.ds(pl.multiple_of(c * tok, tok), tok)
    other_rows = pl.ds(pl.multiple_of((1 - c) * tok, tok), tok)
    load_x = pltpu.make_async_copy(x_ref, xb.at[own_rows], loc.at[0])
    swap_x = pltpu.make_async_remote_copy(x_ref, xb.at[own_rows], d2d_s.at[0], d2d_r.at[0], device_id={"cp": partner})

    def load_wqkv(layer):
        w_q, w_k, w_v = wqkv_src[layer]
        return (pltpu.make_async_copy(w_q.at[:, pl.ds(pl.multiple_of(c * half, hd), half)], wqkv.at[:, pl.ds(0, half)], loc.at[5]),
                pltpu.make_async_copy(w_k.at[:, pl.ds(pl.multiple_of(c * hd, hd), hd)], wqkv.at[:, pl.ds(half, hd)], loc.at[6]),
                pltpu.make_async_copy(w_v.at[:, pl.ds(pl.multiple_of(c * hd, hd), hd)], wqkv.at[:, pl.ds(half + hd, hd)], loc.at[7]))

    def load_wo(layer):
        return pltpu.make_async_copy(wo_src[layer], wob, loc.at[8])

    def load_ff(tile, slot):
        cols = pl.ds(pl.multiple_of(c * ff_half + tile * FF_TILE, 128), FF_TILE)
        return (pltpu.make_async_copy(wg.at[:, cols], w13.at[slot, :, pl.ds(0, FF_TILE)], wsem.at[slot, 0]),
                pltpu.make_async_copy(wu.at[:, cols], w13.at[slot, :, pl.ds(FF_TILE, FF_TILE)], wsem.at[slot, 1]),
                pltpu.make_async_copy(wd.at[cols], w2b.at[slot], wsem.at[slot, 2]))


    hops = (None, (0, near), (4, near), (5, near), (0, mate), (1, mate))

    def pair_copy(slot, order):
        src, target = hops[slot]
        piece = parity(c + order)
        return pltpu.make_async_remote_copy(kv1.at[src, piece], kv1.at[slot, piece], pair_s.at[slot, order],
                                            pair_r.at[slot, order], device_id=chip(target))

    def pair_new(slot):
        src, target = hops[slot]
        return pltpu.make_async_remote_copy(nk1.at[src], nk1.at[slot], pair_s.at[slot, 2], pair_r.at[slot, 2], device_id=chip(target))

    def relay(slot, order, onto):
        pair_copy(slot, order).wait_recv()
        pair_copy(onto, order).start()

    def relay_new(slot, onto):
        pair_new(slot).wait_recv()
        pair_new(onto).start()

    swap_q = pltpu.make_async_remote_copy(qb.at[0], qb.at[1], pair_s.at[0, 0], pair_r.at[0, 0], device_id=chip(mate))
    swap_acc = pltpu.make_async_remote_copy(acc.at[1], far_acc, pair_s.at[0, 1], pair_r.at[0, 1], device_id=chip(mate))
    swap_ml = pltpu.make_async_remote_copy(part_ml, far_ml, pair_s.at[0, 2], pair_r.at[0, 2], device_id=chip(mate))

    def piece_of(t):
        dist = lax.div(t, 4) + 1
        r = lax.rem(t, 4)
        direction = parity(t)
        order = halve(r) + parity(r) * lax.div(dist, far)
        src = lax.rem(z + nz + dist * (2 * direction - 1), nz)
        return src, parity(c + order), direction

    def ring_copy(src, piece, t, direction):
        return pltpu.make_async_remote_copy(kv2.at[src, piece], kv2.at[src, piece], ring_s.at[t], ring_r.at[t],
                                            device_id=toward(direction))

    def send_own(direction, order):
        ring_copy(z, parity(c + order), 2 * order + direction, direction).start()

    def arrive(t):
        src, piece, direction = piece_of(t)
        ring_copy(src, piece, t, direction).wait_recv()
        last = 4 * (far - 1)

        @pl.when((t < last - 4) | (t == last - 4) | (t == last - 1))
        def _():
            ring_copy(src, piece, t + 4 - 2 * lax.div(t, last - 1), direction).start()

    def new_piece(u):
        dist = halve(u) + 1
        direction = parity(u)
        return lax.rem(z + dist * (2 * direction - 1) + nz, nz), direction

    def new_copy(src, u, direction):
        return pltpu.make_async_remote_copy(nk2.at[src], nk2.at[src], new_s.at[u], new_r.at[u], device_id=toward(direction))

    def attend(group, keys_values, causal=False):
        k_view, v_view = keys_values.at[0], keys_values.at[1]
        keys = k_view.shape[0]
        kb = min(256, keys)
        blocks = keys // kb

        def scores(h):
            top = None
            for b in range(blocks):
                s = product(k_view[b * kb:(b + 1) * kb], qb[group, h])
                if causal:
                    key = lax.broadcasted_iota(jnp.int32, s.shape, 0) + b * kb
                    query = lax.broadcasted_iota(jnp.int32, s.shape, 1)
                    s = jnp.where(key <= query, s, -jnp.inf)
                sbuf[h % 2, b * kb:(b + 1) * kb] = s
                part = jnp.max(s.reshape(kb // 8, 8, pair), axis=0)
                top = part if top is None else jnp.maximum(top, part)
            return top

        top = scores(0)
        for h in range(heads_dev):
            top_next = scores(h + 1) if h + 1 < heads_dev else None
            m_old = m_s[group, h]
            m_new = jnp.maximum(m_old, jnp.max(top, axis=0, keepdims=True))
            alpha = jnp.exp2((m_old - m_new) * score_mul)
            total = l_s[group, h] * alpha
            added = None
            for b in range(blocks):
                s = sbuf[h % 2, b * kb:(b + 1) * kb].reshape(kb // 8, 8, pair)
                p = jnp.exp2((s - m_new[None]) * score_mul)
                total = total + jnp.sum(p, axis=0)
                v_t = jnp.concatenate([v_view[b * kb + i * hd:b * kb + (i + 1) * hd] for i in range(kb // hd)], axis=1)
                part = product(v_t, p.reshape(kb, pair).astype(BF16))
                added = part if added is None else added + part
            acc[group, h] = (acc[group, h].reshape(hd // 8, 8, pair) * alpha[None]).reshape(hd, pair) + added
            l_s[group, h] = total
            m_s[group, h] = m_new
            top = top_next

    def new_arrive(u):
        src, direction = new_piece(u)
        new_copy(src, u, direction).wait_recv()

        @pl.when((u < n_new - 3) | (u == n_new - 3))
        def _():
            new_copy(src, u + 2, direction).start()

        @pl.when(src < z)
        def _():
            attend(0, nk2.at[src])

    def clear(groups):
        def one(i, carry):
            group, h = lax.div(i, heads_dev), lax.rem(i, heads_dev)
            m_s[group, h] = jnp.full(m_s.shape[2:], -jnp.inf, F32)
            l_s[group, h] = jnp.zeros(l_s.shape[2:], F32)
            acc[group, h] = jnp.zeros(acc.shape[2:], F32)
            return carry
        repeat(groups * heads_dev, one)

    def rope(vals):
        rounded = vals.astype(BF16).astype(F32)
        return rounded * cos_ref[...] + pltpu.roll(rounded, hd // 2, 1) * sin_ref[...]

    def rotation():
        base = base_rot[z]
        cos_ref[...] = base[0:1] * local_rot[0] - base[1:2] * local_rot[1]
        sin_ref[...] = base[3:4] * local_rot[0] + base[2:3] * local_rot[1]

    def project(layer):
        proj = product(xb[...], wqkv[...])
        start = layer * (bias_ref.shape[0] // 2)
        for h in range(heads_dev):
            cols = slice(h * hd, (h + 1) * hd)
            qb[0, h] = rope(proj[:, cols] + bias_ref[pl.ds(start + c * heads_dev + h, 1)]).T.astype(BF16)
        k_rot = rope(proj[:, half:half + hd] + bias_ref[pl.ds(start + 2 * heads_dev + c, 1)]).astype(BF16)
        own_new(layer)[0] = k_rot
        knew[layer] = k_rot
        v_val = proj[:, half + hd:]
        vnew[layer] = v_val.astype(BF16)
        for i in range(pair // hd):
            own_new(layer)[1, i * hd:(i + 1) * hd] = v_val[i * hd:(i + 1) * hd].T.astype(BF16)

    def append_swap(layer, j):
        return pltpu.make_async_remote_copy((knew, vnew)[j].at[layer, other_rows], app_in.at[layer, j],
                                            d2d_s.at[8 + 2 * layer + j], d2d_r.at[8 + 2 * layer + j], device_id={"cp": partner})

    def send_append(layer):
        for j in range(CORES):
            append_swap(layer, j).start()

    def put_append(layer):
        return pltpu.make_async_copy(app_buf.at[layer], app_out.at[layer], loc.at[9 + layer])

    def append(layer):
        for j in range(CORES):
            append_swap(layer, j).wait_recv()
            mine = (knew, vnew)[j][layer, own_rows].astype(F32)
            theirs = app_in[layer, j].astype(F32)
            wide[pl.ds(0, tok, stride=2)] = jnp.where(c == 0, mine, theirs)
            wide[pl.ds(1, tok, stride=2)] = jnp.where(c == 0, theirs, mine)
            app_buf[layer, j] = wide[pl.ds(0, 2 * tok)].astype(BF16)
        put_append(layer).start()

    def finish_heads(layer):
        for h in range(heads_dev):
            total = jnp.sum(l_s[0, h], axis=0, keepdims=True)
            summed = acc[0, h]
            if layer == 0:
                m_own, m_far = m_s[0, h, 0:1], far_ml[h:h + 1]
                m_all = jnp.maximum(m_own, m_far)
                w_own, w_far = jnp.exp2((m_own - m_all) * score_mul), jnp.exp2((m_far - m_all) * score_mul)
                total = total * w_own + far_ml[8 + h:9 + h] * w_far
                summed = summed * w_own + far_acc[h] * w_far
            ob[layer, c, :, h * hd:(h + 1) * hd] = (summed / total).T.astype(BF16)

    def hand_back():
        for h in range(heads_dev):
            part_ml[h:h + 1] = m_s[1, h, 0:1]
            part_ml[8 + h:9 + h] = jnp.sum(l_s[1, h], axis=0, keepdims=True)
        swap_acc.start()
        swap_ml.start()

    def attend_first():
        def step(k, carry):
            @pl.when(k == 2)
            def _():
                relay(1, 0, 5)
                relay(4, 0, 2)
                relay_new(1, 5)
                relay_new(4, 2)

            @pl.when(k == 3)
            def _():
                swap_q.wait_recv()

            @pl.when(k == 6)
            def _():
                relay(1, 1, 5)

            @pl.when(k == 8)
            def _():
                relay(4, 1, 2)
                pair_copy(2, 0).wait_recv()

            @pl.when(k == 10)
            def _():
                relay(5, 0, 3)
                pair_copy(2, 1).wait_recv()
                pair_new(2).wait_recv()
                relay_new(5, 3)

            @pl.when(k == 12)
            def _():
                relay(5, 1, 3)
                for direction in (odd, 1 - odd):
                    for order in range(CORES):
                        send_own(direction, order)

            @pl.when(k == 14)
            def _():
                pair_new(3).wait_recv()

            @pl.when((k == 12) | (k == 14))
            def _():
                turn = halve(k - 12)

                def new_step(i, carry):
                    slot, group = halve(i), parity(i)
                    src = lax.rem(z + nz + slot * (2 * odd - 1), nz)

                    @pl.when(src < (1 - group) * z + group * mate)
                    def _():
                        attend(group, nk1.at[slot])
                    return carry
                lax.fori_loop(6 * turn, 6 + 2 * turn, new_step, 0)

            @pl.when(k == 12)
            def _():
                pair_copy(3, 0).wait_recv()

            @pl.when(k == 14)
            def _():
                pair_copy(3, 1).wait_recv()

            @pl.when(k == 15)
            def _():
                hand_back()

            early = 1 - lax.div(k + 10, 16)
            i, end = lax.rem(k, 3), lax.div(k, 12)
            slot = early * halve(i) + (1 - early) * lax.div(k, 4)
            order = early * parity(i) + (1 - early) * lax.rem(halve(k), 2)
            group = early * lax.div(k, 3) + (1 - early) * (parity(k) * (1 - 2 * end) + end)
            piece = parity(c + order)
            attend(group, kv1.at[slot, piece])
            return carry

        repeat(16, step)

    def attend_second():
        def step(s, carry):
            @pl.when((s == 2) | (s == 3))
            def _():
                arrive(s + 4)

            @pl.when((s == 8) | (s == 9))
            def _():
                arrive(s)

            @pl.when(s >= 12)
            def _():
                arrive(s - 2)
            own = 1 - lax.div(s + n_steps - 2, n_steps)
            src, piece, _ = piece_of(lax.rem(s + n_steps - 2, n_steps))
            src = own * z + (1 - own) * src
            piece = own * parity(c + s) + (1 - own) * piece
            attend(0, kv2.at[src, piece])

            @pl.when((s == 5) | (s == 11) | (s == 13) | (s == n_steps - 1))
            def _():
                last = lax.div(s, n_steps - 1)
                lo = (s - 9) * lax.div(s, 11)

                def new_step(u, carry):
                    new_arrive(u)
                    return carry
                lax.fori_loop(lo, lo + 2 - last, new_step, 0)
            return carry

        repeat(n_steps, step)

    def span(body, lo, hi):
        def step(i, carry):
            body(i)
            return carry
        lax.fori_loop(lo, hi, step, 0)

    for j in range(CORES):
        load_cache(0, j).start()
    load_x.start()
    for cpy in load_wqkv(0):
        cpy.start()
    barrier = pltpu.get_barrier_semaphore()
    for other in (partner, 2 * mate + c, 2 * near + c):
        pl.semaphore_signal(barrier, inc=1, device_id={"cp": other})
    for j in range(CORES):
        load_cache(0, j).wait()
    split_cache(0)
    pl.semaphore_wait(barrier, 3)
    for slot in (1, 4):
        pair_copy(slot, 0).start()
    swap_cache(0).start()
    swap_x.start()
    for j in range(CORES):
        load_cache(1, j).start()
    rotation()
    load_x.wait()
    swap_x.wait_recv()
    for cpy in load_wqkv(0):
        cpy.wait()
    project(0)
    for slot in (1, 4):
        pair_new(slot).start()
    swap_q.start()
    swap_cache(0).wait_recv()
    for slot in (1, 4):
        pair_copy(slot, 1).start()
    send_append(0)
    load_wo(0).start()
    for cpy in load_wqkv(1):
        cpy.start()
    for slot in range(W_SLOTS):
        for cpy in load_ff(slot, slot):
            cpy.start()
    clear(2)
    attend(0, nk1.at[0], causal=True)
    for j in range(CORES):
        load_cache(1, j).wait()
    split_cache(1)
    swap_cache(1).start()
    append(0)
    swap_cache(1).wait_recv()
    attend_first()
    span(arrive, 0, 2)
    swap_acc.wait_recv()
    swap_ml.wait_recv()
    finish_heads(0)

    swap_o = pltpu.make_async_remote_copy(ob.at[0, c], ob.at[0, c], d2d_s.at[5], d2d_r.at[5], device_id={"cp": partner})
    swap_o.start()
    load_wo(0).wait()
    swap_o.wait_recv()
    y_one = (product(ob[0, 0], wob[:half])
             + product(ob[0, 1], wob[half:])).astype(BF16)
    h_val = (xb[...].astype(F32) + y_one.astype(F32)).astype(BF16)
    hb[...] = h_val
    xb[...] = rms_norm(h_val.astype(F32))
    load_wo(1).start()
    gacc[...] = jnp.zeros(gacc.shape, F32)

    def ff_step(i, carry):
        slot = lax.rem(i, W_SLOTS)
        for cpy in load_ff(i, slot):
            cpy.wait()
        both = product(xb[...], w13[slot]).astype(BF16).astype(F32)
        gate = both[:, :FF_TILE]
        mixed = (gate * jax.nn.sigmoid(gate) * both[:, FF_TILE:]).astype(BF16)
        gacc[...] += product(mixed, w2b[slot])

        @pl.when(i == tiles - 3)
        def _():
            span(arrive, 2, 4)

        @pl.when(i + W_SLOTS < tiles)
        def _():
            for cpy in load_ff(i + W_SLOTS, slot):
                cpy.start()
        return carry

    repeat(tiles, ff_step)
    swap_g = pltpu.make_async_remote_copy(gacc, grecv, d2d_s.at[7], d2d_r.at[7], device_id={"cp": partner})
    swap_g.start()
    span(arrive, 4, 6)
    swap_g.wait_recv()
    g_val = (hb[...].astype(F32) + (gacc[...] + grecv[...])).astype(BF16)
    hb[...] = g_val
    put_g = pltpu.make_async_copy(hb.at[own_rows], g_out, loc.at[11])
    put_g.start()
    xb[...] = rms_norm(g_val.astype(F32))
    for cpy in load_wqkv(1):
        cpy.wait()
    swap_q.wait_send()
    project(1)
    for direction in range(CORES):
        new_copy(z, direction, direction).start()
    send_append(1)

    clear(1)
    attend(0, nk2.at[z], causal=True)
    append(1)
    attend_second()
    finish_heads(1)
    swap_y = pltpu.make_async_remote_copy(ob.at[1, c, other_rows], ob.at[1, c, other_rows], d2d_s.at[6], d2d_r.at[6],
                                          device_id={"cp": partner})
    swap_y.start()
    load_wo(1).wait()
    swap_y.wait_recv()
    ybuf[...] = (product(ob[1, 0, own_rows], wob[:half])
                 + product(ob[1, 1, own_rows], wob[half:])).astype(BF16)
    put_y = pltpu.make_async_copy(ybuf, y_out, loc.at[12])
    put_y.start()

    for layer in range(CORES):
        put_append(layer).wait()
        swap_cache(layer).wait_send()
        for j in range(CORES):
            append_swap(layer, j).wait_send()
    span(lambda t: ring_copy(0, 0, t, 0).wait_send(), 0, n_arr)
    span(lambda u: new_copy(0, u, 0).wait_send(), 0, n_new)
    for slot in range(1, 6):
        for order in range(CORES):
            pair_copy(slot, order).wait_send()
        pair_new(slot).wait_send()
    swap_acc.wait_send()
    swap_ml.wait_send()
    swap_x.wait_send()
    swap_o.wait_send()
    swap_g.wait_send()
    swap_y.wait_send()
    put_g.wait()
    put_y.wait()


def rotation_tables(n, tok, cache_dev, hd):
    half_dim = hd // 2
    inv_freq = np.tile(ROPE_THETA ** (-np.arange(half_dim) * (2.0 / hd)), 2)
    pair = CORES * tok
    offset = np.arange(pair)[:, None] * inv_freq[None, :]
    base = (n * cache_dev + np.arange(n // 2) * pair)[:, None] * inv_freq[None, :]
    sign = np.where(np.arange(hd) < half_dim, -1.0, 1.0)[None, :]
    local_rot = np.stack([np.cos(offset), np.sin(offset)])
    base_rot = np.stack([np.cos(base), np.sin(base), sign * np.cos(base), sign * np.sin(base)], axis=1)
    return jnp.asarray(local_rot, F32), jnp.asarray(base_rot, F32)


def copy_kernel(g_in, y_in, app_in, g_out, y_out, *rest):
    app_outs, (g_buf, y_buf, app_buf, sems) = rest[:4], rest[4:]
    ins = [pltpu.make_async_copy(src, buf, sems.at[0, i]) for i, (src, buf) in enumerate(((y_in, y_buf), (g_in, g_buf), (app_in, app_buf)))]
    outs = [[pltpu.make_async_copy(y_buf, y_out, sems.at[1, 0])], [pltpu.make_async_copy(g_buf, g_out, sems.at[1, 1])],
            [pltpu.make_async_copy(app_buf.at[i // 2, i % 2], app_outs[i], sems.at[1, 2 + i]) for i in range(4)]]
    for cpy in ins:
        cpy.start()
    for cpy, group in zip(ins, outs):
        cpy.wait()
        for out in group:
            out.start()
    for group in outs:
        for out in group:
            out.wait()


def hand_over(hidden, y_two, app):
    any_spec = pl.BlockSpec(memory_space=pl.ANY)
    row_shape = jax.ShapeDtypeStruct(hidden.shape, hidden.dtype)
    app_shape = jax.ShapeDtypeStruct(app.shape[2:], app.dtype)
    return pl.pallas_call(
        copy_kernel,
        out_shape=[row_shape, row_shape] + [app_shape] * 4,
        in_specs=[any_spec] * 3,
        out_specs=[any_spec] * 6,
        scratch_shapes=[pltpu.VMEM(hidden.shape, BF16), pltpu.VMEM(hidden.shape, BF16), pltpu.VMEM(app.shape, BF16),
                        pltpu.SemaphoreType.DMA((2, 6))],
        name="hand_over",
    )(hidden, y_two, app)


def fused_blocks(n, x_in, cache, weights, biases, tables):
    tok, d_model = x_in.shape
    cache_dev, kv_heads, hd = cache[0].shape
    w_q1, w_gate = weights[0], weights[4]
    heads_dev = w_q1.shape[1] // hd // kv_heads
    half = heads_dev * hd
    nz = n // CORES
    far = nz // CORES
    n_arr = 4 * (far - 1) + 2
    n_new = 2 * (far - 1) + 1
    pair = CORES * tok
    rows = [arr.reshape(cache_dev * kv_heads, hd) for arr in cache]
    any_spec = pl.BlockSpec(memory_space=pl.ANY)
    vmem_spec = pl.BlockSpec(memory_space=pltpu.VMEM)
    dma = pltpu.SemaphoreType.DMA
    ff_half = w_gate.shape[1] // 2
    flops = 2 * pair * (d_model * (half + 2 * hd) * 2 + 3 * d_model * ff_half + 2 * half * d_model * 2) + 8 * pair * half * n * cache_dev
    return pl.pallas_call(
        functools.partial(block_kernel, n),
        out_shape=(jax.ShapeDtypeStruct((tok, d_model), BF16), jax.ShapeDtypeStruct((tok, d_model), BF16),
                   jax.ShapeDtypeStruct((2, 2, kv_heads * tok, hd), BF16)),
        in_specs=[any_spec] * 16 + [vmem_spec] * 3,
        out_specs=(any_spec, any_spec, any_spec),
        scratch_shapes=[
            pltpu.VMEM((6, 2, 2, cache_dev, hd), BF16),
            pltpu.VMEM((nz, 2, 2, cache_dev, hd), BF16),
            pltpu.VMEM((6, 2, pair, hd), BF16),
            pltpu.VMEM((nz, 2, pair, hd), BF16),
            pltpu.VMEM((16, pair), F32),
            pltpu.VMEM((heads_dev, hd, pair), F32),
            pltpu.VMEM((16, pair), F32),
            pltpu.VMEM((CORES, CORES, 2 * cache_dev, hd), BF16),
            pltpu.VMEM((CORES, CORES, cache_dev, hd), BF16),
            pltpu.VMEM((2 * hd, hd), F32),
            pltpu.VMEM((CORES, cache_dev, pair), F32),
            pltpu.VMEM((pair, hd), F32),
            pltpu.VMEM((pair, hd), F32),
            pltpu.VMEM((CORES, pair, hd), BF16),
            pltpu.VMEM((CORES, pair, hd), BF16),
            pltpu.VMEM((CORES, CORES, tok, hd), BF16),
            pltpu.VMEM((CORES, CORES, pair, hd), BF16),
            pltpu.VMEM((pair, d_model), BF16),
            pltpu.VMEM((pair, d_model), BF16),
            pltpu.VMEM((CORES, heads_dev, hd, pair), BF16),
            pltpu.VMEM((CORES, heads_dev, hd, pair), F32),
            pltpu.VMEM((CORES, heads_dev, 8, pair), F32),
            pltpu.VMEM((CORES, heads_dev, 8, pair), F32),
            pltpu.VMEM((CORES, CORES, pair, half), BF16),
            pltpu.VMEM((pair, d_model), F32),
            pltpu.VMEM((pair, d_model), F32),
            pltpu.VMEM((tok, d_model), BF16),
            pltpu.VMEM((d_model, half + 2 * hd), BF16),
            pltpu.VMEM((2 * half, d_model), BF16),
            pltpu.VMEM((W_SLOTS, d_model, 2 * FF_TILE), BF16),
            pltpu.VMEM((W_SLOTS, FF_TILE, d_model), BF16),
            dma((6, 3)), dma((6, 3)), dma((n_arr,)), dma((n_arr,)), dma((n_new,)), dma((n_new,)),
            dma((12,)), dma((12,)), dma((13,)), dma((W_SLOTS, 3)),
        ],
        compiler_params=pltpu.CompilerParams(collective_id=0, has_side_effects=True, vmem_limit_bytes=67043328),
        cost_estimate=pl.CostEstimate(flops=flops, bytes_accessed=6 * d_model * ff_half, transcendentals=0),
        name="fused_blocks",
    )(x_in, *rows, *weights, biases, *tables)


def solution(mesh):
    axis_size = mesh.shape['cp']
    rows_spec = P(('dp', 'cp'), None)
    cache_spec = P(('dp', 'cp'), None, None)
    mat_spec = P(None, None)
    vec_spec = P(None)
    layer_specs = (cache_spec, cache_spec, mat_spec, vec_spec, mat_spec, vec_spec, mat_spec, mat_spec)
    in_specs = (rows_spec,) + layer_specs + (mat_spec, mat_spec, mat_spec) + layer_specs
    out_specs = (rows_spec, rows_spec, cache_spec, cache_spec, cache_spec, cache_spec)

    def forward(x_in, cache_k1, cache_v1, w_q1, b_q1, w_k1, b_k1, w_v1, w_o1, w_gate, w_up, w_down, cache_k2, cache_v2, w_q2, b_q2, w_k2, b_k2, w_v2, w_o2):
        tok = x_in.shape[0]
        cache_dev, kv_heads, hd = cache_k1.shape
        tables = rotation_tables(axis_size, tok, cache_dev, hd)
        parts = (b_q1, b_k1, b_q2, b_k2)
        width = sum(part.shape[0] for part in parts)
        biases, start = 0.0, 0
        for part in parts:
            biases = biases + jnp.pad(part.astype(F32), (start, width - start - part.shape[0]))
            start += part.shape[0]
        biases = lax.optimization_barrier(biases).reshape(-1, hd)
        weights = (w_q1, w_k1, w_v1, w_o1, w_gate, w_up, w_down, w_q2, w_k2, w_v2, w_o2)
        hidden, y_two, app = fused_blocks(axis_size, x_in, (cache_k1, cache_v1, cache_k2, cache_v2), weights, biases, tables)
        outs = hand_over(hidden, y_two, app)
        return (outs[0], outs[1], *(arr.reshape(tok, kv_heads, hd) for arr in outs[2:]))

    return jax.shard_map(forward, mesh=mesh, in_specs=in_specs, out_specs=out_specs, check_vma=False)
```

time: 204 us -> 195 us (0.956)
  Pallas kernels: 202 us -> 192 us
    pallas_call x1, Pallas kernels: 200 us -> 190 us  [fused_blocks(): pl.pallas_call(functools.partial(block_kernel, n), out_shape=(jax.ShapeDt...]
where the time goes in v2:
time: 195 us
  Pallas kernels  192 us (98%)
    pallas_call x1, Pallas kernels, fused_blocks(): pl.pallas_call(functools.partial(block_kernel, n), out_shape=(jax.ShapeDt...  190 us

profile of v2, /device:TPU:21, one launch (start us, length us, event | category | flops | bytes accessed | tf_op | source)
XLA Modules:
  0.0 194.6 jit_solution(2181270659781937190)
XLA Ops:
  0.6 1.3 convert_add_fusion
  2.0 190.4 %fused_blocks.1 = (bf16[128,1536]{1,0:T(8,128)(2,1)}, bf16[128,1536]{1,0:T(8,128)(2,1)}, bf16[2,2,256,128]{3,2,1,0:T(8,128)(2,1)}) custom-call(bf16[128,1536]{1,0:T(8,128)(2,1)} %x_ref.1, bf16[2048,128]{1,0:T(8,128)(2,1)} %bitcast.10, bf16[2048,128]{1,0:T(8,128)(2,1)} %bitcast.11, bf16[2048,128]{1,0:T(8,128)(2,1)} %bitcast.12, bf16[2048,128]{1,0:T(8,128)(2,1)} %bitcast.13, ...), custom_call_target="tpu_custom_call" | custom-call | flops 40365981696 | bytes 41287680 | tf_op jit(solution)/shard_map/fused_blocks/pallas_call | solution.py:617
  192.4 2.1 %hand_over.1 = (bf16[128,1536]{1,0:T(8,128)(2,1)}, bf16[128,1536]{1,0:T(8,128)(2,1)}, bf16[256,128]{1,0:T(8,128)(2,1)}, bf16[256,128]{1,0:T(8,128)(2,1)}, bf16[2...) custom-call(bf16[128,1536]{1,0:T(8,128)(2,1)} %get-tuple-element.15.g_in, bf16[128,1536]{1,0:T(8,128)(2,1)} %get-tuple-element.16.y_in, ...), custom_call_target="tpu_custom_call" | custom-call | tf_op jit(solution)/shard_map/hand_over/pallas_call | solution.py:589

commit v3 on v2

--- a/solution.py
+++ b/solution.py
@@ -38,7 +38,7 @@
     return (wide * lax.rsqrt(jnp.mean(wide * wide, axis=-1, keepdims=True) + NORM_EPS)).astype(BF16)
 
 
-def block_kernel(n, x_ref, kc1, vc1, kc2, vc2, wq1, wk1, wv1, wo1, wg, wu, wd, wq2, wk2, wv2, wo2, bias_ref, local_rot, base_rot,
+def block_kernel(n, x_ref, kc1, vc1, kc2, vc2, wq1, wk1, wv1, wo1, wg, wu, wd, wq2, wk2, wv2, wo2, bq1, bk1, bq2, bk2, local_rot, base_rot,
                  g_out, y_out, app_out,
                  kv1, kv2, nk1, nk2, part_ml, far_acc, far_ml, raw, snd, wide, sbuf, cos_ref, sin_ref, knew, vnew, app_in, app_buf,
                  xb, hb, qb, acc, m_s, l_s, ob, gacc, grecv, ybuf, wqkv, wob, w13, w2b,
@@ -251,11 +251,14 @@
 
     def project(layer):
         proj = product(xb[...], wqkv[...])
-        start = layer * (bias_ref.shape[0] // 2)
+        q_bias, k_bias = (ref[...].astype(F32) for ref in ((bq1, bk1), (bq2, bk2))[layer])
+
+        def bias_row(table, low, high):
+            return jnp.where(c == 0, table[low:low + 1], table[high:high + 1])
         for h in range(heads_dev):
             cols = slice(h * hd, (h + 1) * hd)
-            qb[0, h] = rope(proj[:, cols] + bias_ref[pl.ds(start + c * heads_dev + h, 1)]).T.astype(BF16)
-        k_rot = rope(proj[:, half:half + hd] + bias_ref[pl.ds(start + 2 * heads_dev + c, 1)]).astype(BF16)
+            qb[0, h] = rope(proj[:, cols] + bias_row(q_bias, h, heads_dev + h)).T.astype(BF16)
+        k_rot = rope(proj[:, half:half + hd] + bias_row(k_bias, 0, 1)).astype(BF16)
         own_new(layer)[0] = k_rot
         knew[layer] = k_rot
         v_val = proj[:, half + hd:]
@@ -382,10 +385,6 @@
 
     def attend_second():
         def step(s, carry):
-            @pl.when((s == 2) | (s == 3))
-            def _():
-                arrive(s + 4)
-
             @pl.when((s == 8) | (s == 9))
             def _():
                 arrive(s)
@@ -399,15 +398,15 @@
             piece = own * parity(c + s) + (1 - own) * piece
             attend(0, kv2.at[src, piece])
 
-            @pl.when((s == 5) | (s == 11) | (s == 13) | (s == n_steps - 1))
+            @pl.when((s == 7) | (s == 13) | (s == n_steps - 1))
             def _():
                 last = lax.div(s, n_steps - 1)
-                lo = (s - 9) * lax.div(s, 11)
+                lo = (s - 11) * lax.div(s, 13)
 
                 def new_step(u, carry):
                     new_arrive(u)
                     return carry
-                lax.fori_loop(lo, lo + 2 - last, new_step, 0)
+                lax.fori_loop(lo, lo + 2 + last, new_step, 0)
             return carry
 
         repeat(n_steps, step)
@@ -490,9 +489,9 @@
         mixed = (gate * jax.nn.sigmoid(gate) * both[:, FF_TILE:]).astype(BF16)
         gacc[...] += product(mixed, w2b[slot])
 
-        @pl.when(i == tiles - 3)
+        @pl.when(i == tiles - 2)
         def _():
-            span(arrive, 2, 4)
+            span(arrive, 4, 6)
 
         @pl.when(i + W_SLOTS < tiles)
         def _():
@@ -500,10 +499,10 @@
                 cpy.start()
         return carry
 
+    span(arrive, 2, 4)
     repeat(tiles, ff_step)
     swap_g = pltpu.make_async_remote_copy(gacc, grecv, d2d_s.at[7], d2d_r.at[7], device_id={"cp": partner})
     swap_g.start()
-    span(arrive, 4, 6)
     swap_g.wait_recv()
     g_val = (hb[...].astype(F32) + (gacc[...] + grecv[...])).astype(BF16)
     hb[...] = g_val
@@ -516,6 +515,7 @@
     project(1)
     for direction in range(CORES):
         new_copy(z, direction, direction).start()
+    span(arrive, 6, 8)
     send_append(1)
 
     clear(1)
@@ -618,7 +618,7 @@
         functools.partial(block_kernel, n),
         out_shape=(jax.ShapeDtypeStruct((tok, d_model), BF16), jax.ShapeDtypeStruct((tok, d_model), BF16),
                    jax.ShapeDtypeStruct((2, 2, kv_heads * tok, hd), BF16)),
-        in_specs=[any_spec] * 16 + [vmem_spec] * 3,
+        in_specs=[any_spec] * 16 + [vmem_spec] * 6,
         out_specs=(any_spec, any_spec, any_spec),
         scratch_shapes=[
             pltpu.VMEM((6, 2, 2, cache_dev, hd), BF16),
@@ -658,7 +658,7 @@
         compiler_params=pltpu.CompilerParams(collective_id=0, has_side_effects=True, vmem_limit_bytes=67043328),
         cost_estimate=pl.CostEstimate(flops=flops, bytes_accessed=6 * d_model * ff_half, transcendentals=0),
         name="fused_blocks",
-    )(x_in, *rows, *weights, biases, *tables)
+    )(x_in, *rows, *weights, *biases, *tables)
 
 
 def solution(mesh):
@@ -675,13 +675,7 @@
         tok = x_in.shape[0]
         cache_dev, kv_heads, hd = cache_k1.shape
         tables = rotation_tables(axis_size, tok, cache_dev, hd)
-        parts = (b_q1, b_k1, b_q2, b_k2)
-        width = sum(part.shape[0] for part in parts)
-        biases, start = 0.0, 0
-        for part in parts:
-            biases = biases + jnp.pad(part.astype(F32), (start, width - start - part.shape[0]))
-            start += part.shape[0]
-        biases = lax.optimization_barrier(biases).reshape(-1, hd)
+        biases = [part.reshape(-1, hd) for part in (b_q1, b_k1, b_q2, b_k2)]
         weights = (w_q1, w_k1, w_v1, w_o1, w_gate, w_up, w_down, w_q2, w_k2, w_v2, w_o2)
         hidden, y_two, app = fused_blocks(axis_size, x_in, (cache_k1, cache_v1, cache_k2, cache_v2), weights, biases, tables)
         outs = hand_over(hidden, y_two, app)

time: 195 us -> 190 us (0.974)
  Pallas kernels: 192 us -> 189 us
    pallas_call x1, Pallas kernels: 190 us -> 187 us  [fused_blocks(): pl.pallas_call(functools.partial(block_kernel, n), out_shape=(jax.ShapeDt...]
where the time goes in v3:
time: 190 us
  Pallas kernels  189 us (99%)
    pallas_call x1, Pallas kernels, fused_blocks(): pl.pallas_call(functools.partial(block_kernel, n), out_shape=(jax.ShapeDt...  187 us

profile of v3, /device:TPU:21, one launch (start us, length us, event | category | flops | bytes accessed | tf_op | source)
XLA Modules:
  0.0 189.9 jit_solution(16026825867688253847)
XLA Ops:
  0.6 187.0 %fused_blocks.1 = (bf16[128,1536]{1,0:T(8,128)(2,1)}, bf16[128,1536]{1,0:T(8,128)(2,1)}, bf16[2,2,256,128]{3,2,1,0:T(8,128)(2,1)}) custom-call(bf16[128,1536]{1,0:T(8,128)(2,1)} %x_ref.1, bf16[2048,128]{1,0:T(8,128)(2,1)} %bitcast.12, bf16[2048,128]{1,0:T(8,128)(2,1)} %bitcast.13, bf16[2048,128]{1,0:T(8,128)(2,1)} %bitcast.14, bf16[2048,128]{1,0:T(8,128)(2,1)} %bitcast.15, ...), custom_call_target="tpu_custom_call" | custom-call | flops 40365981696 | bytes 41287680 | tf_op jit(solution)/shard_map/fused_blocks/pallas_call | solution.py:617
  187.7 2.1 %hand_over.1 = (bf16[128,1536]{1,0:T(8,128)(2,1)}, bf16[128,1536]{1,0:T(8,128)(2,1)}, bf16[256,128]{1,0:T(8,128)(2,1)}, bf16[256,128]{1,0:T(8,128)(2,1)}, bf16[2...) custom-call(bf16[128,1536]{1,0:T(8,128)(2,1)} %get-tuple-element.15.g_in, bf16[128,1536]{1,0:T(8,128)(2,1)} %get-tuple-element.16.y_in, ...), custom_call_target="tpu_custom_call" | custom-call | tf_op jit(solution)/shard_map/hand_over/pallas_call | solution.py:589

commit v4 on v3

--- a/solution.py
+++ b/solution.py
@@ -398,10 +398,10 @@
             piece = own * parity(c + s) + (1 - own) * piece
             attend(0, kv2.at[src, piece])
 
-            @pl.when((s == 7) | (s == 13) | (s == n_steps - 1))
+            @pl.when((s == 7) | (s == 11) | (s == n_steps - 1))
             def _():
                 last = lax.div(s, n_steps - 1)
-                lo = (s - 11) * lax.div(s, 13)
+                lo = halve(s - 7)
 
                 def new_step(u, carry):
                     new_arrive(u)

time: 190 us -> 191 us (level)
  no operation moved by 1% of the time
where the time goes in v4:
time: 191 us
  Pallas kernels  190 us (99%)
    pallas_call x1, Pallas kernels, fused_blocks(): pl.pallas_call(functools.partial(block_kernel, n), out_shape=(jax.ShapeDt...  188 us

profile of v4, /device:TPU:21, one launch (start us, length us, event | category | flops | bytes accessed | tf_op | source)
XLA Modules:
  0.0 190.9 jit_solution(12072284975296040117)
XLA Ops:
  0.6 188.0 %fused_blocks.1 = (bf16[128,1536]{1,0:T(8,128)(2,1)}, bf16[128,1536]{1,0:T(8,128)(2,1)}, bf16[2,2,256,128]{3,2,1,0:T(8,128)(2,1)}) custom-call(bf16[128,1536]{1,0:T(8,128)(2,1)} %x_ref.1, bf16[2048,128]{1,0:T(8,128)(2,1)} %bitcast.12, bf16[2048,128]{1,0:T(8,128)(2,1)} %bitcast.13, bf16[2048,128]{1,0:T(8,128)(2,1)} %bitcast.14, bf16[2048,128]{1,0:T(8,128)(2,1)} %bitcast.15, ...), custom_call_target="tpu_custom_call" | custom-call | flops 40365981696 | bytes 41287680 | tf_op jit(solution)/shard_map/fused_blocks/pallas_call | solution.py:617
  188.7 2.1 %hand_over.1 = (bf16[128,1536]{1,0:T(8,128)(2,1)}, bf16[128,1536]{1,0:T(8,128)(2,1)}, bf16[256,128]{1,0:T(8,128)(2,1)}, bf16[256,128]{1,0:T(8,128)(2,1)}, bf16[2...) custom-call(bf16[128,1536]{1,0:T(8,128)(2,1)} %get-tuple-element.15.g_in, bf16[128,1536]{1,0:T(8,128)(2,1)} %get-tuple-element.16.y_in, ...), custom_call_target="tpu_custom_call" | custom-call | tf_op jit(solution)/shard_map/hand_over/pallas_call | solution.py:589
